TPU v7x, 32 devices: a whole 2x2x4 slice. The times are simulated.
32 devices in a mesh: sfc: 8 (over z, x), grp: 4 (over y, core).
Axes of the slice: x: 2, y: 2, z: 4, core: 2. Of those that a mesh axis runs over, the one named last changes fastest.
Arguments:
- tracers: float32 [16, 4, 8, 6144], P(None, None, None, ('sfc', 'grp')), may hold values from 0.05 to 60, as said below
- send_counts: int32 [8, 4, 12], P('sfc', 'grp'), may hold values from 1 to 512, 3072 in all within a row
- point_order: int32 [8, 4, 3072], P('sfc', 'grp'), may hold values from 0 to 3071, each once within a row
- depart_elem: int32 [8, 4, 3, 4, 512], P('sfc', 'grp'), may hold values from 0 to 191
- depart_coords: float32 [8, 4, 2, 3, 4, 512], P('sfc', 'grp'), may hold values from -1 to 1
Outputs:
- transported: float32 [16, 4, 8, 6144], P(None, None, None, ('sfc', 'grp'))
Inputs may be any that keep to these rules, and one draw needn't show every extreme that they name: `send_counts`: each row lists, for the 12 owner blocks of one device, how many of its arrival points depart from that owner's elements; a row sums to 3072, and its largest entry is exactly 512. `point_order`: each row is a permutation of the device's arrival points. `tracers`: Positive.
All inputs are finite; a program needn't handle non-finite values.
Results may differ from a plain program's by a relative error of at most 0.0003.
Values sent between devices are 32-bit elements; how exact they have to be, the bound alone decides.
No kernel may reach another device: no remote copies, remote signals or barrier semaphores. Data moves between devices by JAX's collectives and lax.ppermute only.
A program may use at most 64 MiB of HBM per device.

v0:
```python
import jax
import jax.numpy as jnp
from jax import lax
from jax.sharding import PartitionSpec as P

NODE_COORD = (-1.0, -0.4472135954999579, 0.4472135954999579, 1.0)
NODE_WEIGHT = (1.0 / 6.0, 5.0 / 6.0, 5.0 / 6.0, 1.0 / 6.0)


def passed_along(x, axis, by):
    devices = lax.axis_size(axis)
    return lax.ppermute(x, axis, [(i, (i + by) % devices) for i in range(devices)])


def lagrange(coordinate):
    basis_values = []
    for row_node in range(4):
        weighted = jnp.ones_like(coordinate)
        for other_node in range(4):
            if other_node != row_node:
                weighted = weighted * (
                    (coordinate - NODE_COORD[other_node])
                    / (NODE_COORD[row_node] - NODE_COORD[other_node])
                )
        basis_values.append(weighted)
    return basis_values


def interpolate(tracer_field, received):
    source_row = received[0].astype(jnp.int32)
    along_first = lagrange(received[1])
    along_second = lagrange(received[2])
    running_sum = None
    for row_node in range(4):
        for column_node in range(4):
            node_plane = jnp.take(tracer_field[4 * row_node + column_node], source_row, axis=1)
            weighted = (along_first[row_node] * along_second[column_node])[None, :] * node_plane
            if running_sum is None:
                running_sum, lower_bound, upper_bound = (weighted, node_plane, node_plane)
            else:
                running_sum = running_sum + weighted
                lower_bound = jnp.minimum(lower_bound, node_plane)
                upper_bound = jnp.maximum(upper_bound, node_plane)
    return jnp.clip(running_sum, lower_bound, upper_bound)


def quad_table():
    return jnp.array(
        [NODE_WEIGHT[a] * NODE_WEIGHT[b] for a in range(4) for b in range(4)], jnp.float32
    )


def send_across(outgoing, shift_by):
    return passed_along(outgoing, "sfc", shift_by)


def send_back(returned, shift_by):
    return passed_along(returned, "sfc", shift_by)


def local(tracers, send_counts, point_order, depart_elem, depart_coords):
    node_count, levels, tracer_count, element_count = tracers.shape
    channels = levels * tracer_count
    tracer_field = tracers.reshape(node_count, channels, element_count)
    groups = lax.axis_size("grp")
    counts = send_counts.reshape(-1)
    capacity = depart_elem.shape[-1]
    points = node_count * element_count
    offsets = jnp.cumsum(counts) - counts
    slot_index = jnp.arange(capacity, dtype=jnp.int32)
    in_use = slot_index[None, :] < counts[:, None]
    position = jnp.minimum(offsets[:, None] + slot_index[None, :], points - 1)
    target_point = jnp.where(in_use, point_order.reshape(-1)[position], points)
    total_slots = 3 * groups * capacity
    slot_of_point = (
        jnp.zeros((points,), jnp.int32)
        .at[target_point.reshape(-1)]
        .set(jnp.arange(total_slots, dtype=jnp.int32), mode="drop")
    )
    components = [
        depart_elem.reshape(1, 3, groups, capacity).astype(jnp.float32),
        depart_coords.reshape(2, 3, groups, capacity),
    ]
    payload = jnp.concatenate(components, 0)
    stacked = jnp.stack(
        [send_across(payload[:, 0], -1), payload[:, 1], send_across(payload[:, 2], 1)], 1
    )
    arrived = lax.all_to_all(stacked, "grp", split_axis=2, concat_axis=2, tiled=True)
    flat_arrived = arrived.reshape(arrived.shape[0], -1)
    values = interpolate(tracer_field, flat_arrived)
    returned = lax.all_to_all(
        values.reshape(channels, 3, groups, capacity),
        "grp",
        split_axis=2,
        concat_axis=2,
        tiled=True,
    )
    collected = jnp.stack(
        [send_back(returned[:, 0], 1), returned[:, 1], send_back(returned[:, 2], -1)], 1
    )
    flat_collected = collected.reshape(channels, total_slots)
    slot_table = slot_of_point.reshape(node_count, element_count)
    limited = jnp.stack(
        [jnp.take(flat_collected, slot_table[node], axis=1) for node in range(16)], 0
    )
    quadrature = quad_table()
    old_part = jnp.sum(jnp.sum(tracer_field, axis=2) * quadrature[:, None], axis=0)
    new_part = jnp.sum(jnp.sum(limited, axis=2) * quadrature[:, None], axis=0)
    old_mass, new_mass = lax.psum((old_part, new_part), ("sfc", "grp"))
    corrected = limited * (old_mass / new_mass)[None, :, None]
    return corrected.reshape(node_count, levels, tracer_count, element_count)


def solution(mesh):
    in_specs = (
        P(None, None, None, ("sfc", "grp")),
        P("sfc", "grp", None),
        P("sfc", "grp", None),
        P("sfc", "grp", None, None, None),
        P("sfc", "grp", None, None, None, None),
    )
    out_specs = P(None, None, None, ("sfc", "grp"))
    return jax.shard_map(local, mesh=mesh, in_specs=in_specs, out_specs=out_specs, check_vma=False)
```

profile of v0, /device:TPU:0, one launch (start us, length us, event | category | flops | bytes accessed | tf_op | source)
XLA Modules:
  0.0 632.6 jit_solution(7937689852683287153)
XLA Ops:
  1.7 3.0 collective-permute-start.1
  4.7 3.1 collective-permute-start
  10.5 34.3 %gather_fusion = s32[6144]{0:T(1024)S(1)} fusion(s32[3072]{0:T(1024)S(1)} %bitcast.419, s32[6144]{0:T(1024)S(1)} %broadcast_clamp_fusion), kind=kCustom, calls=%fused_computation.32 | custom fusion | bytes 73728 | tf_op jit(solution)/shard_map/gather | solution.py:73
  44.9 23.0 %scatter_custom_fusion = s32[3072]{0:T(1024)S(1)} fusion(s32[6144]{0:T(1024)S(1)} %bitcast.461, s32[6144]{0:T(1024)S(1)} %iota.10, s32[]{:T(128)} %constant.89.clone.1), kind=kCustom, calls=%fused_computation.230 | custom fusion | bytes 12292 | tf_op jit(solution)/shard_map/scatter | solution.py:78
  69.9 3.3 all-to-all-start
  75.4 2.0 all-to-all-done
  78.9 20.9 %gather_fusion.1 = f32[6144,32]{1,0:T(8,128)} fusion(f32[32,192]{0,1:T(8,128)S(1)} %copy.350, s32[6144]{0:T(1024)S(1)} %fusion.23), kind=kCustom, calls=%fused_computation.clone | custom fusion | bytes 1597440 | tf_op jit(solution)/shard_map/jit(_take)/gather | solution.py:36
  99.8 2.3 copy.351
  102.1 20.9 %gather_fusion.2 = f32[6144,32]{1,0:T(8,128)} fusion(f32[32,192]{0,1:T(8,128)S(1)} %copy.352, s32[6144]{0:T(1024)S(1)} %fusion.23), kind=kCustom, calls=%fused_computation.2.clone | custom fusion | bytes 1597440 | tf_op jit(solution)/shard_map/jit(_take)/gather | solution.py:36
  123.1 2.3 copy.353
  125.4 20.9 %gather_fusion.3 = f32[6144,32]{1,0:T(8,128)} fusion(f32[32,192]{0,1:T(8,128)S(1)} %copy.354, s32[6144]{0:T(1024)S(1)} %fusion.23), kind=kCustom, calls=%fused_computation.3.clone | custom fusion | bytes 1597440 | tf_op jit(solution)/shard_map/jit(_take)/gather | solution.py:36
  146.3 3.1 copy.355
  149.4 20.9 %gather_fusion.4 = f32[6144,32]{1,0:T(8,128)} fusion(f32[32,192]{0,1:T(8,128)S(1)} %copy.356, s32[6144]{0:T(1024)S(1)} %fusion.23), kind=kCustom, calls=%fused_computation.4.clone | custom fusion | bytes 1597440 | tf_op jit(solution)/shard_map/jit(_take)/gather | solution.py:36
  170.3 3.1 copy.357
  173.4 20.9 %gather_fusion.5 = f32[6144,32]{1,0:T(8,128)} fusion(f32[32,192]{0,1:T(8,128)S(1)} %copy.358, s32[6144]{0:T(1024)S(1)} %fusion.23), kind=kCustom, calls=%fused_computation.5.clone | custom fusion | bytes 1597440 | tf_op jit(solution)/shard_map/jit(_take)/gather | solution.py:36
  194.3 3.1 copy.359
  197.4 20.9 %gather_fusion.6 = f32[6144,32]{1,0:T(8,128)} fusion(f32[32,192]{0,1:T(8,128)S(1)} %copy.360, s32[6144]{0:T(1024)S(1)} %fusion.23), kind=kCustom, calls=%fused_computation.6.clone | custom fusion | bytes 1597440 | tf_op jit(solution)/shard_map/jit(_take)/gather | solution.py:36
  218.3 3.1 copy.361
  221.4 20.9 %gather_fusion.7 = f32[6144,32]{1,0:T(8,128)} fusion(f32[32,192]{0,1:T(8,128)S(1)} %copy.362, s32[6144]{0:T(1024)S(1)} %fusion.23), kind=kCustom, calls=%fused_computation.7.clone | custom fusion | bytes 1597440 | tf_op jit(solution)/shard_map/jit(_take)/gather | solution.py:36
  242.4 3.1 copy.363
  245.4 20.9 %gather_fusion.8 = f32[6144,32]{1,0:T(8,128)} fusion(f32[32,192]{0,1:T(8,128)S(1)} %copy.364, s32[6144]{0:T(1024)S(1)} %fusion.23), kind=kCustom, calls=%fused_computation.8.clone | custom fusion | bytes 1597440 | tf_op jit(solution)/shard_map/jit(_take)/gather | solution.py:36
  266.4 3.1 copy.365
  269.5 20.9 %gather_fusion.9 = f32[6144,32]{1,0:T(8,128)} fusion(f32[32,192]{0,1:T(8,128)S(1)} %copy.366, s32[6144]{0:T(1024)S(1)} %fusion.23), kind=kCustom, calls=%fused_computation.9.clone | custom fusion | bytes 1597440 | tf_op jit(solution)/shard_map/jit(_take)/gather | solution.py:36
  290.4 3.1 copy.367
  293.5 20.9 %gather_fusion.10 = f32[6144,32]{1,0:T(8,128)} fusion(f32[32,192]{0,1:T(8,128)S(1)} %copy.368, s32[6144]{0:T(1024)S(1)} %fusion.23), kind=kCustom, calls=%fused_computation.10.clone | custom fusion | bytes 1597440 | tf_op jit(solution)/shard_map/jit(_take)/gather | solution.py:36
  314.4 3.1 copy.369
  317.5 20.9 %gather_fusion.11 = f32[6144,32]{1,0:T(8,128)} fusion(f32[32,192]{0,1:T(8,128)S(1)} %copy.370, s32[6144]{0:T(1024)S(1)} %fusion.23), kind=kCustom, calls=%fused_computation.11.clone | custom fusion | bytes 1597440 | tf_op jit(solution)/shard_map/jit(_take)/gather | solution.py:36
  338.4 3.1 copy.371
  341.5 20.9 %gather_fusion.12 = f32[6144,32]{1,0:T(8,128)} fusion(f32[32,192]{0,1:T(8,128)S(1)} %copy.372, s32[6144]{0:T(1024)S(1)} %fusion.23), kind=kCustom, calls=%fused_computation.12.clone | custom fusion | bytes 1597440 | tf_op jit(solution)/shard_map/jit(_take)/gather | solution.py:36
  362.4 3.1 copy.373
  365.5 20.9 %gather_fusion.13 = f32[6144,32]{1,0:T(8,128)} fusion(f32[32,192]{0,1:T(8,128)S(1)} %copy.374, s32[6144]{0:T(1024)S(1)} %fusion.23), kind=kCustom, calls=%fused_computation.13.clone | custom fusion | bytes 1597440 | tf_op jit(solution)/shard_map/jit(_take)/gather | solution.py:36
  386.4 3.1 copy.375
  389.5 20.9 %gather_fusion.14 = f32[6144,32]{1,0:T(8,128)} fusion(f32[32,192]{0,1:T(8,128)S(1)} %copy.376, s32[6144]{0:T(1024)S(1)} %fusion.23), kind=kCustom, calls=%fused_computation.14.clone | custom fusion | bytes 1597440 | tf_op jit(solution)/shard_map/jit(_take)/gather | solution.py:36
  410.4 3.1 copy.377
  413.5 20.9 %gather_fusion.15 = f32[6144,32]{1,0:T(8,128)} fusion(f32[32,192]{0,1:T(8,128)S(1)} %copy.378, s32[6144]{0:T(1024)S(1)} %fusion.23), kind=kCustom, calls=%fused_computation.15.clone | custom fusion | bytes 1597440 | tf_op jit(solution)/shard_map/jit(_take)/gather | solution.py:36
  434.4 3.1 copy.379
  437.5 20.9 %gather_fusion.16 = f32[6144,32]{1,0:T(8,128)} fusion(f32[32,192]{0,1:T(8,128)S(1)} %copy.380, s32[6144]{0:T(1024)S(1)} %fusion.23), kind=kCustom, calls=%fused_computation.16.clone | custom fusion | bytes 1597440 | tf_op jit(solution)/shard_map/jit(_take)/gather | solution.py:36
  458.4 3.2 copy.381
  461.9 5.1 fusion
  468.8 3.5 all-to-all-start.1
  475.7 8.2 %all-to-all-done.1 = f32[32,3,4,512]{3,0,1,2:T(8,128)S(1)} async-done(((f32[32,3,4,512]{3,0,1,2:T(8,128)}), f32[32,3,4,512]{3,0,1,2:T(8,128)S(1)}, u32[]{:S(2)}, u32[]{:S(2)}) %all-to-all-start.1) | async-done | bytes 786464 | tf_op jit(solution)/shard_map/all_to_all | solution.py:91
  484.0 4.7 collective-permute-start.3
  490.6 4.5 collective-permute-done.2
  495.2 2.4 collective-permute-done.3
  498.6 2.0 copy.385
  508.9 1.6 select_bitcast_fusion.24
  510.5 1.6 copy.406
  513.5 1.7 select_bitcast_fusion.22
  515.1 1.6 copy.407
  518.1 1.7 select_bitcast_fusion.20
  522.8 1.7 select_bitcast_fusion.18
  527.4 1.7 select_bitcast_fusion.16
  529.1 1.6 copy.410
  532.1 1.7 select_bitcast_fusion.14
  536.8 1.7 select_bitcast_fusion.12
  538.4 1.6 copy.412
  541.4 1.7 select_bitcast_fusion.10
  546.1 1.7 select_bitcast_fusion.8
  547.7 1.6 copy.414
  550.7 1.7 select_bitcast_fusion.6
  552.4 1.6 copy.415
  555.4 1.7 select_bitcast_fusion.4
  560.0 1.7 select_bitcast_fusion.2
  587.8 38.7 %all-reduce = (f32[32]{0:T(128)S(1)}, f32[32]{0:T(128)S(1)}) all-reduce(f32[32]{0:T(128)} %reduce_sum.40, f32[32]{0:T(128)S(1)} %multiply_reduce_fusion.1), channel_id=1, replica_groups=mesh['sfc'=8,'grp'=4] {'sfc','grp'}, use_global_device_ids=true, to_apply=%region_4.7 | all-reduce | flops 64 | bytes 512 | tf_op jit(solution)/shard_map/psum | solution.py:109
  (223 shorter events, 81.8 us)
Async XLA Ops:
  0.0 10.4 %copy-start = (s32[1,1,3072]{2,1,0:T(1,128)S(1)}, s32[1,1,3072]{2,1,0:T(1,128)}, u32[]{:S(2)}) copy-start(s32[1,1,3072]{2,1,0:T(1,128)} %param.12) | copy-start | bytes 36868
  1.7 67.6 %collective-permute-start.1 = (f32[3,4,512]{2,0,1:T(4,128)S(1)}, f32[3,4,512]{2,0,1:T(4,128)S(1)}, u32[]{:S(2)}, u32[]{:S(2)}) collective-permute-start(f32[3,4,512]{2,0,1:T(4,128)S(1)} %get-tuple-element.64), channel_id=1, source_target_pairs={{0,4},{4,8},{8,12},{12,16},{16,20},{20,24},{24,28},{28,0},{1,5},{5... | collective-permute-start | bytes 73736 | tf_op jit(solution)/shard_map/ppermute | solution.py:12
  4.7 64.5 %collective-permute-start = (f32[3,4,512]{2,0,1:T(4,128)S(1)}, f32[3,4,512]{2,0,1:T(4,128)S(1)}, u32[]{:S(2)}, u32[]{:S(2)}) collective-permute-start(f32[3,4,512]{2,0,1:T(4,128)S(1)} %get-tuple-element.63), channel_id=1, source_target_pairs={{0,28},{4,0},{8,4},{12,8},{16,12},{20,16},{24,20},{28,24},{1,29},{... | collective-permute-start | bytes 73736 | tf_op jit(solution)/shard_map/ppermute | solution.py:12
  10.5 34.3 %copy-start.32 = (s32[1,1,12]{2,1,0:T(1,128)S(1)}, s32[1,1,12]{2,1,0:T(1,128)}, u32[]{:S(2)}) copy-start(s32[1,1,12]{2,1,0:T(1,128)} %param.11) | copy-start | bytes 148
  69.9 7.6 %all-to-all-start = ((f32[3,3,4,512]{3,0,1,2:T(4,128)}), f32[3,3,4,512]{3,0,1,2:T(4,128)S(1)}, u32[]{:S(2)}, u32[]{:S(2)}) async-start(f32[3,3,4,512]{3,0,1,2:T(4,128)} %pad_maximum_fusion.1), calls=%async_computation | async-start | bytes 196608 | tf_op jit(solution)/shard_map/all_to_all | solution.py:88
  458.4 3.2 copy-start.11
  458.4 3.4 copy-start.2
  467.0 5.3 copy-start.22
  467.0 5.3 copy-start.23
  467.0 5.9 copy-start.3
  467.0 6.2 copy-start.20
  467.0 6.2 copy-start.21
  467.0 6.8 %copy-start.18 = (s32[192]{0:T(256)S(1)}, s32[192]{0:T(256)}, u32[]{:S(2)}) copy-start(s32[192]{0:T(256)} %get-tuple-element.104) | copy-start | bytes 2308
  467.1 6.8 %copy-start.19 = (s32[192]{0:T(256)S(1)}, s32[192]{0:T(256)}, u32[]{:S(2)}) copy-start(s32[192]{0:T(256)} %get-tuple-element.105) | copy-start | bytes 2308
  467.1 7.3 %copy-start.16 = (s32[192]{0:T(256)S(1)}, s32[192]{0:T(256)}, u32[]{:S(2)}) copy-start(s32[192]{0:T(256)} %get-tuple-element.102) | copy-start | bytes 2308
  467.1 7.3 %copy-start.17 = (s32[192]{0:T(256)S(1)}, s32[192]{0:T(256)}, u32[]{:S(2)}) copy-start(s32[192]{0:T(256)} %get-tuple-element.103) | copy-start | bytes 2308
  467.1 7.9 %copy-start.14 = (s32[192]{0:T(256)S(1)}, s32[192]{0:T(256)}, u32[]{:S(2)}) copy-start(s32[192]{0:T(256)} %get-tuple-element.100) | copy-start | bytes 2308
  467.1 7.9 %copy-start.15 = (s32[192]{0:T(256)S(1)}, s32[192]{0:T(256)}, u32[]{:S(2)}) copy-start(s32[192]{0:T(256)} %get-tuple-element.101) | copy-start | bytes 2308
  467.1 8.5 %copy-start.31 = (f32[16]{0:T(128)S(1)}, f32[16]{0:T(128)}, u32[]{:S(2)}) copy-start(f32[16]{0:T(128)} %constant.93.clone) | copy-start | bytes 196
  467.1 21.6 %copy-start.12 = (s32[192]{0:T(256)S(1)}, s32[192]{0:T(256)}, u32[]{:S(2)}) copy-start(s32[192]{0:T(256)} %get-tuple-element.98) | copy-start | bytes 2308
  467.1 21.6 %copy-start.13 = (s32[192]{0:T(256)S(1)}, s32[192]{0:T(256)}, u32[]{:S(2)}) copy-start(s32[192]{0:T(256)} %get-tuple-element.99) | copy-start | bytes 2308
  468.8 15.1 %all-to-all-start.1 = ((f32[32,3,4,512]{3,0,1,2:T(8,128)}), f32[32,3,4,512]{3,0,1,2:T(8,128)S(1)}, u32[]{:S(2)}, u32[]{:S(2)}) async-start(f32[32,3,4,512]{3,0,1,2:T(8,128)} %copy.384), calls=%async_computation.1 | async-start | bytes 1572864 | tf_op jit(solution)/shard_map/all_to_all | solution.py:91
  484.0 11.2 %collective-permute-start.2 = (f32[32,4,512]{2,0,1:T(8,128)S(1)}, f32[32,4,512]{2,0,1:T(8,128)S(1)}, u32[]{:S(2)}, u32[]{:S(2)}) collective-permute-start(f32[32,4,512]{2,0,1:T(8,128)S(1)} %get-tuple-element.9), channel_id=1, source_target_pairs={{0,4},{4,8},{8,12},{12,16},{16,20},{20,24},{24,28},{28,0},{1,5},{5... | collective-permute-start | bytes 786440 | tf_op jit(solution)/shard_map/ppermute | solution.py:12
  484.0 13.6 %collective-permute-start.3 = (f32[32,4,512]{2,0,1:T(8,128)S(1)}, f32[32,4,512]{2,0,1:T(8,128)S(1)}, u32[]{:S(2)}, u32[]{:S(2)}) collective-permute-start(f32[32,4,512]{2,0,1:T(8,128)S(1)} %get-tuple-element.10), channel_id=1, source_target_pairs={{0,28},{4,0},{8,4},{12,8},{16,12},{20,16},{24,20},{28,24},{1,29},{... | collective-permute-start | bytes 786440 | tf_op jit(solution)/shard_map/ppermute | solution.py:12
  498.6 10.2 %copy-start.30 = (pred[192]{0:T(512)(128)(4,1)S(1)}, pred[192]{0:T(512)(128)(4,1)}, u32[]{:S(2)}) copy-start(pred[192]{0:T(512)(128)(4,1)} %get-tuple-element.94) | copy-start | bytes 580
  498.6 14.9 %copy-start.29 = (pred[192]{0:T(512)(128)(4,1)S(1)}, pred[192]{0:T(512)(128)(4,1)}, u32[]{:S(2)}) copy-start(pred[192]{0:T(512)(128)(4,1)} %get-tuple-element.93) | copy-start | bytes 580
  498.6 19.5 %copy-start.28 = (pred[192]{0:T(512)(128)(4,1)S(1)}, pred[192]{0:T(512)(128)(4,1)}, u32[]{:S(2)}) copy-start(pred[192]{0:T(512)(128)(4,1)} %get-tuple-element.92) | copy-start | bytes 580
  510.5 40.3 %copy-start.27 = (pred[192]{0:T(512)(128)(4,1)S(1)}, pred[192]{0:T(512)(128)(4,1)}, u32[]{:S(2)}) copy-start(pred[192]{0:T(512)(128)(4,1)} %get-tuple-element.85) | copy-start | bytes 580
  515.1 40.2 %copy-start.26 = (pred[192]{0:T(512)(128)(4,1)S(1)}, pred[192]{0:T(512)(128)(4,1)}, u32[]{:S(2)}) copy-start(pred[192]{0:T(512)(128)(4,1)} %get-tuple-element.84) | copy-start | bytes 580
  519.8 40.2 %copy-start.25 = (pred[192]{0:T(512)(128)(4,1)S(1)}, pred[192]{0:T(512)(128)(4,1)}, u32[]{:S(2)}) copy-start(pred[192]{0:T(512)(128)(4,1)} %get-tuple-element.83) | copy-start | bytes 580
  524.4 40.4 %copy-start.24 = (pred[192]{0:T(512)(128)(4,1)S(1)}, pred[192]{0:T(512)(128)(4,1)}, u32[]{:S(2)}) copy-start(pred[192]{0:T(512)(128)(4,1)} %get-tuple-element.82) | copy-start | bytes 580
  563.3 69.3 %copy-start.1 = (s32[1,1,3072]{2,1,0:T(1,128)S(1)}, s32[1,1,3072]{2,1,0:T(1,128)}, u32[]{:S(2)}) copy-start(s32[1,1,3072]{2,1,0:T(1,128)} %param.12) | copy-start | bytes 36868
  564.8 66.0 %copy-start.4 = (f32[32,192]{0,1:T(8,128)S(1)}, f32[32,192]{0,1:T(8,128)}, u32[]{:S(2)}) copy-start(f32[32,192]{0,1:T(8,128)} %get-tuple-element.43) | copy-start | bytes 73732
  564.8 66.1 %copy-start.5 = (f32[32,192]{0,1:T(8,128)S(1)}, f32[32,192]{0,1:T(8,128)}, u32[]{:S(2)}) copy-start(f32[32,192]{0,1:T(8,128)} %get-tuple-element.41) | copy-start | bytes 73732
  564.8 66.1 %copy-start.6 = (f32[32,192]{0,1:T(8,128)S(1)}, f32[32,192]{0,1:T(8,128)}, u32[]{:S(2)}) copy-start(f32[32,192]{0,1:T(8,128)} %get-tuple-element.39) | copy-start | bytes 73732
  564.8 66.2 %copy-start.7 = (f32[32,192]{0,1:T(8,128)S(1)}, f32[32,192]{0,1:T(8,128)}, u32[]{:S(2)}) copy-start(f32[32,192]{0,1:T(8,128)} %get-tuple-element.37) | copy-start | bytes 73732
  564.8 66.3 %copy-start.8 = (f32[32,192]{0,1:T(8,128)S(1)}, f32[32,192]{0,1:T(8,128)}, u32[]{:S(2)}) copy-start(f32[32,192]{0,1:T(8,128)} %get-tuple-element.35) | copy-start | bytes 73732
  564.8 66.4 %copy-start.9 = (f32[32,192]{0,1:T(8,128)S(1)}, f32[32,192]{0,1:T(8,128)}, u32[]{:S(2)}) copy-start(f32[32,192]{0,1:T(8,128)} %get-tuple-element.33) | copy-start | bytes 73732
  564.9 66.4 %copy-start.10 = (f32[32,192]{0,1:T(8,128)S(1)}, f32[32,192]{0,1:T(8,128)}, u32[]{:S(2)}) copy-start(f32[32,192]{0,1:T(8,128)} %get-tuple-element.31) | copy-start | bytes 73732
where the time goes:
time: 636 us; the launch traced here: 633 us
  local copies, waits for them, and re-layouts  516 us (81%)
  other arithmetic  42.6 us (7%)
  blocking collectives  38.7 us (6%)
  starting transfers between devices  17.7 us (3%)
  waiting for transfers between devices  17.2 us (3%)
    gather x32, local copies, waits for them, and re-layouts, interpolate(): jnp.take(tracer_field[4 * row_node + column_node], source_row, axis=1)  383 us
    psum x1, blocking collectives, local(): old_mass, new_mass = lax.psum((old_part, new_part), ('sfc', 'grp'))  38.7 us
    gather x2, local copies, waits for them, and re-layouts, local(): target_point = jnp.where(in_use, point_order.reshape(-1)[position], points)  34.3 us
    scatter x1, local copies, waits for them, and re-layouts, local(): slot_of_point = jnp.zeros((points,), jnp.int32).at[target_point.reshape(-...  23 us
    another operation x16, other arithmetic, local(): jnp.stack([jnp.take(flat_collected, slot_table[node], axis=1) for node in...  22.8 us
    gather x16, local copies, waits for them, and re-layouts, local(): jnp.take(flat_collected, slot_table[node], axis=1)  21.6 us
    unnamed x116, local copies, waits for them, and re-layouts  21.1 us
    another operation x18, local copies, waits for them, and re-layouts, local(): jnp.stack([jnp.take(flat_collected, slot_table[node], axis=1) for node in...  20.9 us
  transfers between devices with their start and end apart: 6, of which 4 were waited for; matrix products, arithmetic and copies ran while one was open for 11% of the time, Pallas kernels for 0%

commit v1 on v0

v1 whole, which is shorter than its diff:
```python
import functools

import jax
import jax.numpy as jnp
from jax import lax
from jax.experimental import pallas as pl
from jax.experimental.pallas import tpu as pltpu
from jax.sharding import PartitionSpec as P

NODE_COORD = (-1.0, -0.4472135954999579, 0.4472135954999579, 1.0)
NODE_WEIGHT = (1.0 / 6.0, 5.0 / 6.0, 5.0 / 6.0, 1.0 / 6.0)
LANES = 128
VMEM = pltpu.MemorySpace.VMEM
SMEM = pltpu.MemorySpace.SMEM


def passed_along(x, axis, by):
    devices = lax.axis_size(axis)
    return lax.ppermute(x, axis, [(i, (i + by) % devices) for i in range(devices)])


def lagrange(coordinate):
    basis_values = []
    for row_node in range(4):
        weighted = jnp.ones_like(coordinate)
        for other_node in range(4):
            if other_node != row_node:
                weighted = weighted * (
                    (coordinate - NODE_COORD[other_node])
                    * (1.0 / (NODE_COORD[row_node] - NODE_COORD[other_node]))
                )
        basis_values.append(weighted)
    return basis_values


def bf16_parts(x):
    high = x.astype(jnp.bfloat16)
    low = (x - high.astype(jnp.float32)).astype(jnp.bfloat16)
    return high, low


def prep_kernel(elements, counts, order, elem, coords, first, middle, last, node_out, elem_out, padded):
    groups, capacity = elem.shape[1:]
    points = order.shape[1]
    padded[:, :points] = jnp.broadcast_to(order[...], (8, points))
    lane = lax.broadcasted_iota(jnp.int32, (8, capacity), 1)
    width = capacity + LANES
    offset = jnp.int32(0)
    for d, out in enumerate((first, middle, last)):
        for h in range(groups):
            k = d * groups + h
            count = counts[k]
            base = pl.multiple_of(lax.shift_left(lax.shift_right_logical(offset, 7), 7), LANES)
            rest = lax.bitwise_and(offset, LANES - 1)
            window = padded[:, pl.ds(base, width)]
            point = pltpu.roll(window, lax.rem(width - rest, width), 1)[:, :capacity]
            used = lane < count
            node = ((point.astype(jnp.float32) + 0.5) * (1.0 / elements)).astype(jnp.int32)
            at_elem = point - node * elements
            row, column = lax.shift_right_logical(node, 2), lax.bitwise_and(node, 3)
            inner_row = (row == 1) | (row == 2)
            inner_column = (column == 1) | (column == 2)
            weight = jnp.where(inner_row, NODE_WEIGHT[1], NODE_WEIGHT[0]) * jnp.where(
                inner_column, NODE_WEIGHT[1], NODE_WEIGHT[0]
            )
            weight = jnp.where(used, weight, 0.0)
            out[h, 0:1, :] = elem[d, h:h + 1, :].astype(jnp.float32)
            out[h, 1:2, :] = coords[0, d, h:h + 1, :]
            out[h, 2:3, :] = coords[1, d, h:h + 1, :]
            out[h, 3:4, :] = weight[0:1, :]
            node_out[d, h:h + 1, :] = jnp.where(used, node, -1)[0:1, :]
            elem_out[d, h:h + 1, :] = jnp.where(used, at_elem, -1)[0:1, :]
            offset = offset + count


def split_kernel(channels, tracers, high_out, low_out, mass_out):
    x = tracers[...]
    high, low = bf16_parts(x)
    high_out[...] = high
    low_out[...] = low
    total = None
    for node in range(16):
        quadrature = NODE_WEIGHT[node // 4] * NODE_WEIGHT[node % 4]
        term = x[node * channels:(node + 1) * channels, :] * quadrature
        total = term if total is None else total + term
    mass_out[...] = jnp.sum(total, axis=1, keepdims=True) + jnp.zeros((channels, LANES), jnp.float32)


def interp_kernel(channels, high, low, old, queries, values, mass, acc):
    groups, sides, _, capacity = queries.shape
    elements = high.shape[1]
    acc[...] = jnp.zeros_like(acc)
    row = lax.broadcasted_iota(jnp.int32, (elements, capacity), 0).astype(jnp.float32)

    def block(k, carry):
        h, d = lax.div(k, sides), lax.rem(k, sides)
        query = queries[h, d]
        onehot = jnp.where(row == query[0:1, :], 1.0, 0.0).astype(jnp.bfloat16)
        field = jnp.dot(high[...], onehot, preferred_element_type=jnp.float32) + jnp.dot(
            low[...], onehot, preferred_element_type=jnp.float32
        )
        along_first = lagrange(query[1:2, :])
        along_second = lagrange(query[2:3, :])
        total = least = greatest = None
        for node in range(16):
            plane = field[node * channels:(node + 1) * channels, :]
            weighted = (along_first[node // 4] * along_second[node % 4]) * plane
            if total is None:
                total, least, greatest = weighted, plane, plane
            else:
                total = total + weighted
                least = jnp.minimum(least, plane)
                greatest = jnp.maximum(greatest, plane)
        value = jnp.minimum(jnp.maximum(total, least), greatest)
        values[h, d] = value
        acc[...] += value * query[3:4, :]
        return carry

    lax.fori_loop(0, groups * sides, block, 0)
    new = jnp.sum(acc[...], axis=1, keepdims=True) + jnp.zeros((channels, LANES), jnp.float32)
    lane = lax.broadcasted_iota(jnp.int32, (channels, LANES), 1)
    which = lax.broadcasted_iota(jnp.int32, (channels, LANES), 0)
    spread = jnp.where(lane == which, old[...], 0.0) + jnp.where(lane == which + channels, new, 0.0)
    mass[...] = jnp.sum(spread, axis=0, keepdims=True)


def final_kernel(channels, first, middle, last, node, elem, masses, out, acc):
    groups, _, capacity = first.shape
    elements = out.shape[1]
    row = lax.broadcasted_iota(jnp.int32, (elements, capacity), 0)
    acc[...] = jnp.zeros_like(acc)
    for d, values in enumerate((first, middle, last)):
        def block(h, carry):
            high, low = bf16_parts(values[h])
            at_node = jnp.broadcast_to(node[d, pl.ds(h, 1), :].astype(jnp.float32), (channels, capacity)).astype(jnp.bfloat16)
            onehot = jnp.where(row == elem[d, pl.ds(h, 1), :], 1.0, 0.0).astype(jnp.bfloat16)
            zero = jnp.zeros_like(high)
            added = None
            for part in (high, low):
                spread = jnp.concatenate(
                    [jnp.where(at_node == float(n), part, zero) for n in range(16)], 0
                )
                term = lax.dot_general(
                    spread, onehot, (((1,), (1,)), ((), ())), preferred_element_type=jnp.float32
                )
                added = term if added is None else added + term
            acc[...] += added
            return carry

        lax.fori_loop(0, groups, block, 0)
    total = jnp.sum(masses[...], axis=0, keepdims=True)
    lane = lax.broadcasted_iota(jnp.int32, (channels, LANES), 1)
    which = lax.broadcasted_iota(jnp.int32, (channels, LANES), 0)
    old = jnp.sum(jnp.where(lane == which, total, 0.0), axis=1, keepdims=True)
    new = jnp.sum(jnp.where(lane == which + channels, total, 0.0), axis=1, keepdims=True)
    ratio = old / new
    for n in range(16):
        rows = slice(n * channels, (n + 1) * channels)
        out[rows, :] = acc[rows, :] * ratio


def whole(memory=VMEM):
    return pl.BlockSpec(memory_space=memory)


def local(tracers, send_counts, point_order, depart_elem, depart_coords):
    node_count, levels, tracer_count, elements = tracers.shape
    channels = levels * tracer_count
    groups = lax.axis_size("grp")
    devices = lax.axis_size("sfc") * groups
    capacity = depart_elem.shape[-1]
    points = node_count * elements
    f32, i32 = jnp.float32, jnp.int32
    shape = jax.ShapeDtypeStruct

    field = tracers.reshape(node_count * channels, elements)
    first, middle, last, node, elem = pl.pallas_call(
        functools.partial(prep_kernel, elements),
        out_shape=[shape((groups, 4, capacity), f32)] * 3 + [shape((3, groups, capacity), i32)] * 2,
        in_specs=[whole(SMEM)] + [whole()] * 3,
        out_specs=[whole()] * 5,
        scratch_shapes=[pltpu.VMEM((8, points + capacity + LANES), i32)],
        name="prep",
    )(
        send_counts.reshape(-1),
        point_order.reshape(1, points),
        depart_elem.reshape(3, groups, capacity),
        depart_coords.reshape(2, 3, groups, capacity),
    )
    high, low, old = pl.pallas_call(
        functools.partial(split_kernel, channels),
        out_shape=[shape(field.shape, jnp.bfloat16)] * 2 + [shape((channels, LANES), f32)],
        in_specs=[whole()],
        out_specs=[whole()] * 3,
        cost_estimate=pl.CostEstimate(flops=4_000_000, bytes_accessed=1_000_000, transcendentals=0),
        name="split",
    )(field)
    stacked = jnp.stack(
        [passed_along(first, "sfc", -1), middle, passed_along(last, "sfc", 1)], 1
    )
    arrived = lax.all_to_all(stacked, "grp", split_axis=0, concat_axis=0, tiled=True)
    values, mass = pl.pallas_call(
        functools.partial(interp_kernel, channels),
        out_shape=[shape((groups, 3, channels, capacity), f32), shape((1, LANES), f32)],
        in_specs=[whole()] * 4,
        out_specs=[whole()] * 2,
        scratch_shapes=[pltpu.VMEM((channels, capacity), f32)],
        name="interp",
    )(high, low, old, arrived)
    returned = lax.all_to_all(values, "grp", split_axis=0, concat_axis=0, tiled=True)
    from_ahead = passed_along(returned[:, 0], "sfc", 1)
    from_behind = passed_along(returned[:, 2], "sfc", -1)
    copies = jnp.broadcast_to(mass[None], (devices, 1, LANES))
    masses = lax.all_to_all(copies, ("sfc", "grp"), split_axis=0, concat_axis=0, tiled=True)
    out = pl.pallas_call(
        functools.partial(final_kernel, channels),
        out_shape=shape(field.shape, f32),
        in_specs=[whole()] * 6,
        out_specs=whole(),
        scratch_shapes=[pltpu.VMEM(field.shape, f32)],
        name="final",
    )(from_ahead, returned[:, 1], from_behind, node, elem, masses.reshape(devices, LANES))
    return out.reshape(tracers.shape)


def solution(mesh):
    in_specs = (
        P(None, None, None, ("sfc", "grp")),
        P("sfc", "grp", None),
        P("sfc", "grp", None),
        P("sfc", "grp", None, None, None),
        P("sfc", "grp", None, None, None, None),
    )
    out_specs = P(None, None, None, ("sfc", "grp"))
    return jax.shard_map(local, mesh=mesh, in_specs=in_specs, out_specs=out_specs, check_vma=False)
```

time: 636 us -> 70.4 us (0.11)
  local copies, waits for them, and re-layouts: 516 us -> 2.87 us
  other arithmetic: 42.6 us -> 1.4 us
  Pallas kernels: 0 us -> 19 us
  blocking collectives: 38.7 us -> 26.2 us
  waiting for transfers between devices: 17.2 us -> 9.12 us
  starting transfers between devices: 17.7 us -> 11.3 us
    gather x50 -> x0, local copies, waits for them, and re-layouts: 439 us -> none  [the longest x32 383 us: interpolate(): jnp.take(tracer_field[4 * row_node + column_node], source_row, axis=1)]
    psum x1 -> x0, blocking collectives: 38.7 us -> none  [local(): old_mass, new_mass = lax.psum((old_part, new_part), ('sfc', 'grp'))]
    all_to_all x0 -> x2, blocking collectives: none -> 26.2 us  [the longest x1 15.1 us: local(): lax.all_to_all(values, 'grp', split_axis=0, concat_axis=0, tiled=True)]
    another operation x19 -> x1, other arithmetic: 25.2 us -> 1.4 us  [local(): jnp.stack([passed_along(first, 'sfc', -1), middle, passed_along(last, 'sf...]
    scatter x1 -> x0, local copies, waits for them, and re-layouts: 23 us -> none  [local(): slot_of_point = jnp.zeros((points,), jnp.int32).at[target_point.reshape(-...]
    another operation x19 -> x0, local copies, waits for them, and re-layouts: 22.9 us -> none  [the longest x18 20.9 us: local(): jnp.stack([jnp.take(flat_collected, slot_table[node], axis=1) for node in...]
    unnamed x116 -> x8, local copies, waits for them, and re-layouts: 21.1 us -> 2.1 us
    pallas_call x0 -> x4, Pallas kernels: none -> 19 us  [the longest x1 7.65 us: local(): pl.pallas_call(functools.partial(interp_kernel, channels), out_shape=[sha...]
  transfers between devices with their start and end apart: 6 -> 5, of which waited for: 4 -> 3; matrix products, arithmetic and copies ran while one was open for 11% -> 0% of each run, Pallas kernels for 0% -> 3%
where the time goes in v1:
time: 70.4 us; the launch traced here: 69.9 us
  blocking collectives  26.2 us (37%)
  Pallas kernels  19 us (27%)
  starting transfers between devices  11.3 us (16%)
  waiting for transfers between devices  9.12 us (13%)
  local copies, waits for them, and re-layouts  2.87 us (4%)
  other arithmetic  1.4 us (2%)
    all_to_all x1, blocking collectives, local(): lax.all_to_all(values, 'grp', split_axis=0, concat_axis=0, tiled=True)  15.1 us
    all_to_all x1, blocking collectives, local(): lax.all_to_all(copies, ('sfc', 'grp'), split_axis=0, concat_axis=0, tiled...  11.1 us
    ppermute x4, starting transfers between devices, passed_along(): lax.ppermute(x, axis, [(i, (i + by) % devices) for i in range(devices)])  8.03 us
    pallas_call x1, Pallas kernels, local(): pl.pallas_call(functools.partial(interp_kernel, channels), out_shape=[sha...  7.65 us
    pallas_call x1, Pallas kernels, local(): pl.pallas_call(functools.partial(final_kernel, channels), out_shape=shape...  7.54 us
    ppermute x4, waiting for transfers between devices, passed_along(): lax.ppermute(x, axis, [(i, (i + by) % devices) for i in range(devices)])  6.82 us
    all_to_all x1, starting transfers between devices, local(): lax.all_to_all(stacked, 'grp', split_axis=0, concat_axis=0, tiled=True)  3.3 us
    all_to_all x1, waiting for transfers between devices, local(): lax.all_to_all(stacked, 'grp', split_axis=0, concat_axis=0, tiled=True)  2.29 us
  transfers between devices with their start and end apart: 5, of which 3 were waited for; matrix products, arithmetic and copies ran while one was open for 0% of the time, Pallas kernels for 3%

profile of v1, /device:TPU:0, one launch (start us, length us, event | category | flops | bytes accessed | tf_op | source)
XLA Modules:
  0.0 69.9 jit_solution(7442222696346480699)
XLA Ops:
  0.0 1.8 %prep.1 = (f32[4,4,512]{2,1,0:T(4,128)}, f32[4,4,512]{2,1,0:T(4,128)}, f32[4,4,512]{2,1,0:T(4,128)}, s32[3,4,512]{2,1,0:T(4,128)}, s32[3,4,512]{2,1,0:T(4,128)}) custom-call(s32[12]{0:T(128)} %bitcast.31, s32[1,3072]{1,0:T(1,128)} %bitcast.30, s32[3,4,512]{2,1,0:T(4,128)} %bitcast.29, f32[2,3,4,512]{3,2,1,0:T(4,128)} %bitcast.25), custom_call_target="tpu_custom_call" | custom-call | tf_op jit(solution)/shard_map/prep/pallas_call | solution.py:177
  1.8 6.0 %collective-permute-start = (f32[4,4,512]{2,1,0:T(4,128)}, f32[4,4,512]{2,1,0:T(4,128)S(1)}, u32[]{:S(2)}, u32[]{:S(2)}) collective-permute-start(f32[4,4,512]{2,1,0:T(4,128)} %get-tuple-element.18), channel_id=1, source_target_pairs={{0,28},{4,0},{8,4},{12,8},{16,12},{20,16},{24,20},{28,24},{1,29},{... | collective-permute-start | bytes 98312 | tf_op jit(solution)/shard_map/ppermute | solution.py:19
  7.8 0.0 collective-permute-start.1
  7.8 1.9 %collective-permute-done = f32[4,4,512]{2,1,0:T(4,128)S(1)} collective-permute-done((f32[4,4,512]{2,1,0:T(4,128)}, f32[4,4,512]{2,1,0:T(4,128)S(1)}, u32[]{:S(2)}, u32[]{:S(2)}) %collective-permute-start) | collective-permute-done | bytes 32800 | tf_op jit(solution)/shard_map/ppermute | solution.py:19
  9.7 4.9 %collective-permute-done.1 = f32[4,4,512]{2,1,0:T(4,128)S(1)} collective-permute-done((f32[4,4,512]{2,1,0:T(4,128)}, f32[4,4,512]{2,1,0:T(4,128)S(1)}, u32[]{:S(2)}, u32[]{:S(2)}) %collective-permute-start.1) | collective-permute-done | bytes 32800 | tf_op jit(solution)/shard_map/ppermute | solution.py:19
  14.6 1.4 %pad_maximum_fusion = f32[4,3,4,512]{3,2,1,0:T(4,128)} fusion(f32[4,1,4,512]{3,2,1,0:T(4,128)S(1)} %bitcast.28, f32[4,1,4,512]{3,2,1,0:T(4,128)} %bitcast.26, f32[4,1,4,512]{3,2,1,0:T(4,128)S(1)} %bitcast.27), kind=kLoop, calls=%fused_computation.3 | loop fusion | flops 49152 | bytes 196608 | tf_op jit(solution)/shard_map/stack | solution.py:198
  16.0 3.3 %all-to-all-start = ((f32[4,3,4,512]{3,2,1,0:T(4,128)}), f32[4,3,4,512]{3,2,1,0:T(4,128)S(1)}, u32[]{:S(2)}, u32[]{:S(2)}) async-start(f32[4,3,4,512]{3,2,1,0:T(4,128)} %pad_maximum_fusion), calls=%async_computation | async-start | bytes 196608 | tf_op jit(solution)/shard_map/all_to_all | solution.py:201
  19.3 2.0 %split.1 = (bf16[512,192]{1,0:T(8,128)(2,1)}, bf16[512,192]{1,0:T(8,128)(2,1)}, f32[32,128]{1,0:T(8,128)}) custom-call(f32[512,192]{1,0:T(8,128)} %bitcast.23), custom_call_target="tpu_custom_call" | custom-call | flops 4000000 | bytes 1000000 | tf_op jit(solution)/shard_map/split/pallas_call | solution.py:190
  21.3 2.3 %all-to-all-done.queries = f32[4,3,4,512]{3,2,1,0:T(4,128)S(1)} async-done(((f32[4,3,4,512]{3,2,1,0:T(4,128)}), f32[4,3,4,512]{3,2,1,0:T(4,128)S(1)}, u32[]{:S(2)}, u32[]{:S(2)}) %all-to-all-start) | async-done | bytes 98336 | tf_op jit(solution)/shard_map/all_to_all | solution.py:201
  23.6 0.0 copy-start
  23.6 0.6 copy-done
  24.2 7.6 %interp.1 = (f32[4,3,32,512]{3,2,1,0:T(8,128)}, f32[1,128]{1,0:T(1,128)}) custom-call(bf16[512,192]{1,0:T(8,128)(2,1)} %get-tuple-element.15.high, bf16[512,192]{1,0:T(8,128)(2,1)} %get-tuple-element.16.low, f32[32,128]{1,0:T(8,128)} %get-tuple-element.17.old, f32[4,3,4,512]{3,2,1,0:T(4,128)} %copy-done), custom_call_target="tpu_custom_call" | custom-call | tf_op jit(solution)/shard_map/interp/pallas_call | solution.py:202
  31.9 15.1 %all_to_all.15 = f32[4,3,32,512]{3,2,1,0:T(8,128)S(1)} all-to-all(f32[4,3,32,512]{3,2,1,0:T(8,128)} %get-tuple-element.21), channel_id=1, replica_groups=mesh['sfc'=8,'grp'=4] {'grp'}, dimensions={0} | all-to-all | bytes 1572864 | tf_op jit(solution)/shard_map/all_to_all | solution.py:210
  47.0 0.8 %slice_bitcast_fusion = (f32[4,32,512]{2,1,0:T(8,128)S(1)}, f32[4,32,512]{2,1,0:T(8,128)}, f32[4,32,512]{2,1,0:T(8,128)S(1)}) fusion(f32[4,3,32,512]{3,2,1,0:T(8,128)S(1)} %all_to_all.15), kind=kLoop, calls=%fused_computation | loop fusion | bytes 1572864 | tf_op jit(solution)/shard_map/squeeze | solution.py:212
  47.7 0.0 collective-permute-start.3
  47.7 2.0 %collective-permute-start.2 = (f32[4,32,512]{2,1,0:T(8,128)S(1)}, f32[4,32,512]{2,1,0:T(8,128)S(1)}, u32[]{:S(2)}, u32[]{:S(2)}) collective-permute-start(f32[4,32,512]{2,1,0:T(8,128)S(1)} %get-tuple-element.27), channel_id=1, source_target_pairs={{0,4},{4,8},{8,12},{12,16},{16,20},{20,24},{24,28},{28,0},{1,5},{5... | collective-permute-start | bytes 786440 | tf_op jit(solution)/shard_map/ppermute | solution.py:19
  49.8 0.0 copy-start.3
  49.8 0.7 copy-done.3
  50.4 11.1 %all_to_all.16 = f32[32,1,128]{2,1,0:T(1,128)} all-to-all(f32[32,1,128]{2,1,0:T(1,128)S(1)} %broadcast_in_dim.9), channel_id=1, replica_groups=mesh['sfc'=8,'grp'=4] {'sfc','grp'}, dimensions={0} | all-to-all | bytes 32768 | tf_op jit(solution)/shard_map/all_to_all | solution.py:214
  61.6 0.0 collective-permute-done.3.last
  61.6 0.0 copy-start.1
  61.6 0.0 collective-permute-done.2.first
  61.6 0.0 copy-start.2
  61.6 0.7 copy-done.1
  62.3 0.1 copy-done.2
  62.4 7.5 %final.1 = f32[512,192]{1,0:T(8,128)} custom-call(f32[4,32,512]{2,1,0:T(8,128)} %copy-done.2, f32[4,32,512]{2,1,0:T(8,128)} %get-tuple-element.26.middle, f32[4,32,512]{2,1,0:T(8,128)} %copy-done.1, s32[3,4,512]{2,1,0:T(4,128)} %get-tuple-element.22.node, s32[3,4,512]{2,1,0:T(4,128)} %get-tuple-element.23.elem, f32[32,128]{1,0:T(8,128)} %bitcast.24), custom_call_target="tpu_custom_call" | custom-call | tf_op jit(solution)/shard_map/final/pallas_call | solution.py:215
  (1 shorter events, 0.0 us)
Async XLA Ops:
  1.8 7.9 %collective-permute-start = (f32[4,4,512]{2,1,0:T(4,128)}, f32[4,4,512]{2,1,0:T(4,128)S(1)}, u32[]{:S(2)}, u32[]{:S(2)}) collective-permute-start(f32[4,4,512]{2,1,0:T(4,128)} %get-tuple-element.18), channel_id=1, source_target_pairs={{0,28},{4,0},{8,4},{12,8},{16,12},{20,16},{24,20},{28,24},{1,29},{... | collective-permute-start | bytes 98312 | tf_op jit(solution)/shard_map/ppermute | solution.py:19
  7.8 6.8 %collective-permute-start.1 = (f32[4,4,512]{2,1,0:T(4,128)}, f32[4,4,512]{2,1,0:T(4,128)S(1)}, u32[]{:S(2)}, u32[]{:S(2)}) collective-permute-start(f32[4,4,512]{2,1,0:T(4,128)} %get-tuple-element.20), channel_id=1, source_target_pairs={{0,4},{4,8},{8,12},{12,16},{16,20},{20,24},{24,28},{28,0},{1,5},{5... | collective-permute-start | bytes 98312 | tf_op jit(solution)/shard_map/ppermute | solution.py:19
  16.0 7.6 %all-to-all-start = ((f32[4,3,4,512]{3,2,1,0:T(4,128)}), f32[4,3,4,512]{3,2,1,0:T(4,128)S(1)}, u32[]{:S(2)}, u32[]{:S(2)}) async-start(f32[4,3,4,512]{3,2,1,0:T(4,128)} %pad_maximum_fusion), calls=%async_computation | async-start | bytes 196608 | tf_op jit(solution)/shard_map/all_to_all | solution.py:201
  23.6 0.6 copy-start
  47.7 13.8 %collective-permute-start.3 = (f32[4,32,512]{2,1,0:T(8,128)S(1)}, f32[4,32,512]{2,1,0:T(8,128)S(1)}, u32[]{:S(2)}, u32[]{:S(2)}) collective-permute-start(f32[4,32,512]{2,1,0:T(8,128)S(1)} %get-tuple-element.25), channel_id=1, source_target_pairs={{0,28},{4,0},{8,4},{12,8},{16,12},{20,16},{24,20},{28,24},{1,29},{... | collective-permute-start | bytes 786440 | tf_op jit(solution)/shard_map/ppermute | solution.py:19
  47.7 13.8 %collective-permute-start.2 = (f32[4,32,512]{2,1,0:T(8,128)S(1)}, f32[4,32,512]{2,1,0:T(8,128)S(1)}, u32[]{:S(2)}, u32[]{:S(2)}) collective-permute-start(f32[4,32,512]{2,1,0:T(8,128)S(1)} %get-tuple-element.27), channel_id=1, source_target_pairs={{0,4},{4,8},{8,12},{12,16},{16,20},{20,24},{24,28},{28,0},{1,5},{5... | collective-permute-start | bytes 786440 | tf_op jit(solution)/shard_map/ppermute | solution.py:19
  49.8 0.7 copy-start.3
  61.6 0.7 %copy-start.1 = (f32[4,32,512]{2,1,0:T(8,128)}, f32[4,32,512]{2,1,0:T(8,128)S(1)}, u32[]{:S(2)}) copy-start(f32[4,32,512]{2,1,0:T(8,128)S(1)} %collective-permute-done.3.last) | copy-start | bytes 786436
  61.6 0.8 %copy-start.2 = (f32[4,32,512]{2,1,0:T(8,128)}, f32[4,32,512]{2,1,0:T(8,128)S(1)}, u32[]{:S(2)}) copy-start(f32[4,32,512]{2,1,0:T(8,128)S(1)} %collective-permute-done.2.first) | copy-start | bytes 786436

commit v2 on v0

v2 whole, which is shorter than its diff:
```python
import functools

import jax
import jax.numpy as jnp
from jax import lax
from jax.experimental import pallas as pl
from jax.experimental.pallas import tpu as pltpu
from jax.sharding import PartitionSpec as P

NODE_COORD = (-1.0, -0.4472135954999579, 0.4472135954999579, 1.0)
NODE_WEIGHT = (1.0 / 6.0, 5.0 / 6.0, 5.0 / 6.0, 1.0 / 6.0)
LANES = 128
VMEM = pltpu.MemorySpace.VMEM
HBM = pltpu.MemorySpace.HBM


def lagrange(coordinate):
    basis_values = []
    for row_node in range(4):
        weighted = jnp.ones_like(coordinate)
        for other_node in range(4):
            if other_node != row_node:
                weighted = weighted * (
                    (coordinate - NODE_COORD[other_node])
                    * (1.0 / (NODE_COORD[row_node] - NODE_COORD[other_node]))
                )
        basis_values.append(weighted)
    return basis_values


def bf16_parts(x):
    high = x.astype(jnp.bfloat16)
    low = (x - high.astype(jnp.float32)).astype(jnp.bfloat16)
    return high, low


def prep_kernel(elements, counts_in, order_in, elem_in, coords_in, *rest):
    groups, capacity = elem_in.shape[1:]
    chips = groups // 2
    messages, rest = rest[:3 * chips], rest[3 * chips:]
    node_out, elem_out, padded, starts, counts, order, elem, coords, sems = rest
    arrivals = [
        pltpu.make_async_copy(source, target, sems.at[i])
        for i, (source, target) in enumerate(
            ((counts_in, counts), (order_in, order), (elem_in, elem), (coords_in, coords))
        )
    ]
    for arrival in arrivals:
        arrival.start()
    for arrival in arrivals:
        arrival.wait()
    points = order.shape[1]
    padded[:, :points] = jnp.broadcast_to(order[...], (8, points))
    offset = jnp.int32(0)
    for k in range(3 * groups):
        starts[k] = offset
        offset = offset + counts[0, k]
    odd = lax.bitwise_and(lax.axis_index("sfc"), 1)
    me = lax.axis_index("grp")
    chip, core = lax.shift_right_logical(me, 1), lax.bitwise_and(me, 1)
    sides = (2 * odd, 2 - 2 * odd, 1)
    lane = lax.broadcasted_iota(jnp.int32, (8, capacity), 1)
    width = capacity + LANES
    for stage, d in enumerate(sides):
        for hop in range(chips):
            target = lax.rem(chip + hop, chips)
            message = messages[stage * chips + hop]
            for half in range(2):
                h = target * 2 + lax.bitwise_xor(core, half)
                k = d * groups + h
                first, count = starts[k], counts[0, k]
                base = pl.multiple_of(lax.shift_left(lax.shift_right_logical(first, 7), 7), LANES)
                skip = lax.bitwise_and(first, LANES - 1)
                window = padded[:, pl.ds(base, width)]
                point = pltpu.roll(window, lax.rem(width - skip, width), 1)[:, :capacity]
                used = lane < count
                node = ((point.astype(jnp.float32) + 0.5) * (1.0 / elements)).astype(jnp.int32)
                at_elem = point - node * elements
                row, column = lax.shift_right_logical(node, 2), lax.bitwise_and(node, 3)
                inner_row = (row == 1) | (row == 2)
                inner_column = (column == 1) | (column == 2)
                weight = jnp.where(inner_row, NODE_WEIGHT[1], NODE_WEIGHT[0]) * jnp.where(
                    inner_column, NODE_WEIGHT[1], NODE_WEIGHT[0]
                )
                weight = jnp.where(used, weight, 0.0)
                message[half, 0:1, :] = elem[d, pl.ds(h, 1), :].astype(jnp.float32)
                message[half, 1:2, :] = coords[0, d, pl.ds(h, 1), :]
                message[half, 2:3, :] = coords[1, d, pl.ds(h, 1), :]
                message[half, 3:4, :] = weight[0:1, :]
                slot = 2 * hop + half
                node_out[stage, slot:slot + 1, :] = jnp.where(used, node, -1)[0:1, :]
                elem_out[stage, slot:slot + 1, :] = jnp.where(used, at_elem, -1)[0:1, :]


def split_kernel(channels, mine_in, other, high_out, low_out, mass_out, mine, sem):
    arrival = pltpu.make_async_copy(mine_in, mine, sem)
    arrival.start()
    high_out[1], low_out[1] = bf16_parts(other[...])
    arrival.wait()
    high_out[0], low_out[0] = bf16_parts(mine[...])
    total = None
    for node in range(16):
        quadrature = NODE_WEIGHT[node // 4] * NODE_WEIGHT[node % 4]
        term = mine[node * channels:(node + 1) * channels, :] * quadrature
        total = term if total is None else total + term
    mass_out[...] = jnp.sum(total, axis=1, keepdims=True) + jnp.zeros((channels, LANES), jnp.float32)


def lane_sums(x):
    return sum(x[:, i:i + LANES] for i in range(0, x.shape[1], LANES))


def interp_kernel(channels, messages, last, high, low, carried, *rest):
    queries, rest = rest[:messages], rest[messages:]
    if last:
        old, *outs, mass = rest
    else:
        *outs, mass = rest
    elements = high.shape[2]
    capacity = queries[0].shape[-1]
    row = lax.broadcasted_iota(jnp.int32, (elements, capacity), 0).astype(jnp.float32)
    new = carried[...] if carried is not None else jnp.zeros((channels, LANES), jnp.float32)
    for query_ref, out in zip(queries, outs):
        for half in range(2):
            query = query_ref[half]
            onehot = jnp.where(row == query[0:1, :], 1.0, 0.0).astype(jnp.bfloat16)
            field = jnp.dot(high[half], onehot, preferred_element_type=jnp.float32) + jnp.dot(
                low[half], onehot, preferred_element_type=jnp.float32
            )
            along_first = lagrange(query[1:2, :])
            along_second = lagrange(query[2:3, :])
            total = least = greatest = None
            for node in range(16):
                plane = field[node * channels:(node + 1) * channels, :]
                weighted = (along_first[node // 4] * along_second[node % 4]) * plane
                if total is None:
                    total, least, greatest = weighted, plane, plane
                else:
                    total = total + weighted
                    least = jnp.minimum(least, plane)
                    greatest = jnp.maximum(greatest, plane)
            value = jnp.minimum(jnp.maximum(total, least), greatest)
            out[half] = value
            new = new + lane_sums(value * query[3:4, :])
    if not last:
        mass[...] = new
        return
    new = jnp.sum(new, axis=1, keepdims=True) + jnp.zeros((channels, LANES), jnp.float32)
    lane = lax.broadcasted_iota(jnp.int32, (channels, LANES), 1)
    which = lax.broadcasted_iota(jnp.int32, (channels, LANES), 0)
    spread = jnp.where(lane == which, old[...], 0.0) + jnp.where(lane == which + channels, new, 0.0)
    mass[...] = jnp.broadcast_to(jnp.sum(spread, axis=0, keepdims=True), mass.shape)


def scattered(channels, value_refs, node, elem, elements):
    capacity = value_refs[0].shape[-1]
    row = lax.broadcasted_iota(jnp.int32, (elements, capacity), 0)
    total = None
    for i, values in enumerate(value_refs):
        for half in range(2):
            slot = 2 * i + half
            at_node = jnp.broadcast_to(
                node[slot:slot + 1, :].astype(jnp.float32), (channels, capacity)
            ).astype(jnp.bfloat16)
            onehot = jnp.where(row == elem[slot:slot + 1, :], 1.0, 0.0).astype(jnp.bfloat16)
            for part in bf16_parts(values[half]):
                zero = jnp.zeros_like(part)
                spread = jnp.concatenate(
                    [jnp.where(at_node == float(n), part, zero) for n in range(16)], 0
                )
                term = lax.dot_general(
                    spread, onehot, (((1,), (1,)), ((), ())), preferred_element_type=jnp.float32
                )
                total = term if total is None else total + term
    return total


def scatter_kernel(channels, stage, messages, *rest):
    values, (node, elem), rest = rest[:messages], rest[messages:messages + 2], rest[messages + 2:]
    *carried, out = rest
    total = scattered(channels, values, node.at[stage], elem.at[stage], out.shape[1])
    out[...] = total + carried[0][...] if carried else total


def scale_kernel(channels, carried, masses, out):
    total = jnp.sum(masses[...], axis=0, keepdims=True)
    lane = lax.broadcasted_iota(jnp.int32, (channels, LANES), 1)
    which = lax.broadcasted_iota(jnp.int32, (channels, LANES), 0)
    old = jnp.sum(jnp.where(lane == which, total, 0.0), axis=1, keepdims=True)
    new = jnp.sum(jnp.where(lane == which + channels, total, 0.0), axis=1, keepdims=True)
    ratio = old / new
    for n in range(16):
        rows = slice(n * channels, (n + 1) * channels)
        out[rows, :] = carried[rows, :] * ratio


def whole(memory=VMEM):
    return pl.BlockSpec(memory_space=memory)


def call(kernel, name, out_shape, *args, outside=0, scratch=(), flops=1_000_000):
    outs = out_shape if isinstance(out_shape, (list, tuple)) else [out_shape]
    moved = sum(x.size * x.dtype.itemsize for x in list(args) + list(outs))
    return pl.pallas_call(
        kernel,
        out_shape=out_shape,
        in_specs=[whole(HBM)] * outside + [whole()] * (len(args) - outside),
        out_specs=[whole()] * len(outs) if outs is out_shape else whole(),
        scratch_shapes=list(scratch),
        compiler_params=pltpu.CompilerParams(vmem_limit_bytes=16 * 1024 * 1024),
        cost_estimate=pl.CostEstimate(flops=flops, bytes_accessed=moved, transcendentals=0),
        name=name,
    )(*[pltpu.with_memory_space_constraint(x, HBM) if i < outside else x for i, x in enumerate(args)])


def local(tracers, send_counts, point_order, depart_elem, depart_coords):
    node_count, levels, tracer_count, elements = tracers.shape
    channels = levels * tracer_count
    segments, groups = lax.axis_size("sfc"), lax.axis_size("grp")
    chips = groups // 2
    devices = segments * groups
    capacity = depart_elem.shape[-1]
    points = node_count * elements
    f32, i32 = jnp.float32, jnp.int32
    shape = jax.ShapeDtypeStruct
    both = ("sfc", "grp")

    def route(stage, hop, back=False):
        pairs = []
        for s in range(segments):
            t = ((((s + 1) ^ 1) - 1) % segments, s ^ 1, s)[stage]
            for g in range(groups):
                to = ((g // 2 + hop) % chips) * 2 + g % 2
                pairs.append((s * groups + g, t * groups + to))
        return [(b, a) for a, b in pairs] if back else pairs

    def moved(stage, arrays, back=False):
        return [
            x if stage == 2 and hop == 0 else lax.ppermute(x, both, route(stage, hop, back))
            for hop, x in enumerate(arrays)
        ]

    field = tracers.reshape(node_count * channels, elements)
    *messages, node, elem = call(
        functools.partial(prep_kernel, elements),
        "prep",
        [shape((2, 4, capacity), f32)] * (3 * chips) + [shape((3, groups, capacity), i32)] * 2,
        send_counts.reshape(1, 3 * groups),
        point_order.reshape(1, points),
        depart_elem.reshape(3, groups, capacity),
        depart_coords.reshape(2, 3, groups, capacity),
        outside=4,
        scratch=[
            pltpu.VMEM((8, points + capacity + LANES), i32),
            pltpu.SMEM((3 * groups,), i32),
            pltpu.SMEM((1, 3 * groups), i32),
            pltpu.VMEM((1, points), i32),
            pltpu.VMEM((3, groups, capacity), i32),
            pltpu.VMEM((2, 3, groups, capacity), f32),
            pltpu.SemaphoreType.DMA((4,)),
        ],
    )
    arrived = [moved(stage, messages[stage * chips:(stage + 1) * chips]) for stage in range(3)]
    other = lax.ppermute(field, "grp", [(i, i ^ 1) for i in range(groups)])
    high, low, old = call(
        functools.partial(split_kernel, channels),
        "split",
        [shape((2,) + field.shape, jnp.bfloat16)] * 2 + [shape((channels, LANES), f32)],
        field,
        other,
        outside=1,
        scratch=[pltpu.VMEM(field.shape, f32), pltpu.SemaphoreType.DMA],
    )
    value_shapes = [shape((2, channels, capacity), f32)] * chips
    new = jnp.zeros((channels, LANES), f32)
    returned = []
    for stage in range(3):
        last = stage == 2
        *values, new = call(
            functools.partial(interp_kernel, channels, chips, last),
            f"interp{stage}",
            value_shapes + [shape((devices if last else channels, LANES), f32)],
            high, low, new, *arrived[stage], *([old] if last else []),
            flops=400_000_000,
        )
        returned.append(moved(stage, values, back=True))
    masses = lax.all_to_all(new.reshape(devices, 1, LANES), both, split_axis=0, concat_axis=0, tiled=True)
    so_far = []
    for stage in range(3):
        so_far = [
            call(
                functools.partial(scatter_kernel, channels, stage, chips),
                f"scatter{stage}",
                shape(field.shape, f32),
                *returned[stage], node, elem, *so_far,
                flops=400_000_000,
            )
        ]
    out = call(
        functools.partial(scale_kernel, channels),
        "scale",
        shape(field.shape, f32),
        *so_far, masses.reshape(devices, LANES),
    )
    return out.reshape(tracers.shape)


def solution(mesh):
    in_specs = (
        P(None, None, None, ("sfc", "grp")),
        P("sfc", "grp", None),
        P("sfc", "grp", None),
        P("sfc", "grp", None, None, None),
        P("sfc", "grp", None, None, None, None),
    )
    out_specs = P(None, None, None, ("sfc", "grp"))
    return jax.shard_map(local, mesh=mesh, in_specs=in_specs, out_specs=out_specs, check_vma=False)
```

time: 636 us -> 40.5 us (0.06)
  local copies, waits for them, and re-layouts: 516 us -> 0.01 us
  other arithmetic: 42.6 us -> 0 us
  blocking collectives: 38.7 us -> 0 us
  waiting for transfers between devices: 17.2 us -> 4.67 us
  Pallas kernels: 0 us -> 12.1 us
    gather x50 -> x0, local copies, waits for them, and re-layouts: 439 us -> none  [the longest x32 383 us: interpolate(): jnp.take(tracer_field[4 * row_node + column_node], source_row, axis=1)]
    psum x1 -> x0, blocking collectives: 38.7 us -> none  [local(): old_mass, new_mass = lax.psum((old_part, new_part), ('sfc', 'grp'))]
    another operation x19 -> x0, other arithmetic: 25.2 us -> none  [the longest x16 22.8 us: local(): jnp.stack([jnp.take(flat_collected, slot_table[node], axis=1) for node in...]
    scatter x1 -> x0, local copies, waits for them, and re-layouts: 23 us -> none  [local(): slot_of_point = jnp.zeros((points,), jnp.int32).at[target_point.reshape(-...]
    another operation x19 -> x0, local copies, waits for them, and re-layouts: 22.9 us -> none  [the longest x18 20.9 us: local(): jnp.stack([jnp.take(flat_collected, slot_table[node], axis=1) for node in...]
    unnamed x116 -> x0, local copies, waits for them, and re-layouts: 21.1 us -> none
    pallas_call x0 -> x9, Pallas kernels: none -> 12.1 us  [call(): pl.pallas_call(kernel, out_shape=out_shape, in_specs=[whole(HBM)] * outsi...]
    ppermute x4 -> x11, starting transfers between devices: 10.9 us -> 20 us  [the longest x10 19.5 us: moved(): lax.ppermute(x, both, route(stage, hop, back))]
  transfers between devices with their start and end apart: 6 -> 12, of which waited for: 4 -> 2; matrix products, arithmetic and copies ran while one was open for 11% -> 0% of each run, Pallas kernels for 0% -> 28%
where the time goes in v2:
time: 40.5 us; the launch traced here: 40.3 us
  starting transfers between devices  23.4 us (58%)
  Pallas kernels  12.1 us (30%)
  waiting for transfers between devices  4.67 us (12%)
    ppermute x10, starting transfers between devices, moved(): lax.ppermute(x, both, route(stage, hop, back))  19.5 us
    pallas_call x9, Pallas kernels, call(): pl.pallas_call(kernel, out_shape=out_shape, in_specs=[whole(HBM)] * outsi...  12.1 us
    all_to_all x1, starting transfers between devices, local(): lax.all_to_all(new.reshape(devices, 1, LANES), both, split_axis=0, concat...  3.39 us
    all_to_all x1, waiting for transfers between devices, local(): lax.all_to_all(new.reshape(devices, 1, LANES), both, split_axis=0, concat...  3.17 us
    ppermute x10, waiting for transfers between devices, moved(): lax.ppermute(x, both, route(stage, hop, back))  1.49 us
  transfers between devices with their start and end apart: 12, of which 2 were waited for; matrix products, arithmetic and copies ran while one was open for 0% of the time, Pallas kernels for 28%

profile of v2, /device:TPU:0, one launch (start us, length us, event | category | flops | bytes accessed | tf_op | source)
XLA Modules:
  0.0 40.3 jit_solution(14498802767283680526)
XLA Ops:
  0.0 0.5 %collective-permute-start = (f32[512,192]{1,0:T(8,128)}, f32[512,192]{1,0:T(8,128)S(1)}, u32[]{:S(2)}, u32[]{:S(2)}) collective-permute-start(f32[512,192]{1,0:T(8,128)} %bitcast.11), channel_id=1, source_target_pairs={{0,1},{1,0},{2,3},{3,2},{4,5},{5,4},{6,7},{7,6},{8,9},{9,8},{10,11... | collective-permute-start | bytes 1179656 | tf_op jit(solution)/shard_map/ppermute | solution.py:264
  0.5 1.2 %prep.1 = (f32[2,4,512]{2,1,0:T(4,128)S(1)}, f32[2,4,512]{2,1,0:T(4,128)S(1)}, f32[2,4,512]{2,1,0:T(4,128)S(1)}, f32[2,4,512]{2,1,0:T(4,128)S(1)}, f32[2,4,512]{...) custom-call(s32[1,12]{1,0:T(1,128)} %bitcast.16, ...), custom_call_target="tpu_custom_call" | custom-call | flops 1000000 | bytes 233520 | tf_op jit(solution)/shard_map/prep/pallas_call | solution.py:204
  1.7 5.6 %collective-permute-start.1 = (f32[2,4,512]{2,1,0:T(4,128)S(1)}, f32[2,4,512]{2,1,0:T(4,128)S(1)}, u32[]{:S(2)}, u32[]{:S(2)}) collective-permute-start(f32[2,4,512]{2,1,0:T(4,128)S(1)} %get-tuple-element.27), channel_id=1, source_target_pairs={{0,28},{1,29},{2,30},{3,31},{4,8},{5,9},{6,10},{7,11},{8,4},{9,5},... | collective-permute-start | bytes 49160 | tf_op jit(solution)/shard_map/ppermute | solution.py:239
  7.3 1.1 %collective-permute-start.2 = (f32[2,4,512]{2,1,0:T(4,128)S(1)}, f32[2,4,512]{2,1,0:T(4,128)S(1)}, u32[]{:S(2)}, u32[]{:S(2)}) collective-permute-start(f32[2,4,512]{2,1,0:T(4,128)S(1)} %get-tuple-element.28), channel_id=1, source_target_pairs={{0,30},{1,31},{2,28},{3,29},{4,10},{5,11},{6,8},{7,9},{8,6},{9,7},... | collective-permute-start | bytes 49160 | tf_op jit(solution)/shard_map/ppermute | solution.py:239
  8.4 0.0 collective-permute-start.3
  8.4 1.9 %collective-permute-start.4 = (f32[2,4,512]{2,1,0:T(4,128)S(1)}, f32[2,4,512]{2,1,0:T(4,128)S(1)}, u32[]{:S(2)}, u32[]{:S(2)}) collective-permute-start(f32[2,4,512]{2,1,0:T(4,128)S(1)} %get-tuple-element.31), channel_id=1, source_target_pairs={{0,6},{1,7},{2,4},{3,5},{4,2},{5,3},{6,0},{7,1},{8,14},{9,15},{10,... | collective-permute-start | bytes 49160 | tf_op jit(solution)/shard_map/ppermute | solution.py:239
  10.3 0.0 collective-permute-done.other
  10.3 1.6 %collective-permute-start.5 = (f32[2,4,512]{2,1,0:T(4,128)S(1)}, f32[2,4,512]{2,1,0:T(4,128)S(1)}, u32[]{:S(2)}, u32[]{:S(2)}) collective-permute-start(f32[2,4,512]{2,1,0:T(4,128)S(1)} %get-tuple-element.34), channel_id=1, source_target_pairs={{0,2},{1,3},{2,0},{3,1},{4,6},{5,7},{6,4},{7,5},{8,10},{9,11},{10,... | collective-permute-start | bytes 49160 | tf_op jit(solution)/shard_map/ppermute | solution.py:239
  11.9 1.2 %split.1 = (bf16[2,512,192]{2,1,0:T(8,128)(2,1)S(1)}, bf16[2,512,192]{2,1,0:T(8,128)(2,1)S(1)}, f32[32,128]{1,0:T(8,128)S(1)}) custom-call(f32[512,192]{1,0:T(8,128)} %bitcast.12, f32[512,192]{1,0:T(8,128)S(1)} %collective-permute-done.other), custom_call_target="tpu_custom_call" | custom-call | flops 1000000 | bytes 1589248 | tf_op jit(solution)/shard_map/split/pallas_call | solution.py:204
  13.1 0.0 collective-permute-done.1.rest_0_
  13.1 1.5 %collective-permute-done.2.rest_1_ = f32[2,4,512]{2,1,0:T(4,128)S(1)} collective-permute-done((f32[2,4,512]{2,1,0:T(4,128)S(1)}, f32[2,4,512]{2,1,0:T(4,128)S(1)}, u32[]{:S(2)}, u32[]{:S(2)}) %collective-permute-start.2) | collective-permute-done | bytes 16416 | tf_op jit(solution)/shard_map/ppermute | solution.py:239
  14.6 1.4 %interp0.1 = (f32[2,32,512]{2,1,0:T(8,128)S(1)}, f32[2,32,512]{2,1,0:T(8,128)S(1)}, f32[32,128]{1,0:T(8,128)S(1)}) custom-call(bf16[2,512,192]{2,1,0:T(8,128)(2,1)S(1)} %get-tuple-element.25.high, bf16[2,512,192]{2,1,0:T(8,128)(2,1)S(1)} %get-tuple-element.26.low, f32[32,128]{1,0:T(8,128)S(1)} %broadcast_in_dim.3.carried, ...), custom_call_target="tpu_custom_call" | custom-call | flops 400000000 | bytes 1114112 | tf_op jit(solution)/shard_map/interp0/pallas_call | solution.py:204
  16.0 3.1 %collective-permute-start.9 = (f32[2,32,512]{2,1,0:T(8,128)S(1)}, f32[2,32,512]{2,1,0:T(8,128)S(1)}, u32[]{:S(2)}, u32[]{:S(2)}) collective-permute-start(f32[2,32,512]{2,1,0:T(8,128)S(1)} %get-tuple-element.42), channel_id=1, source_target_pairs={{28,0},{29,1},{30,2},{31,3},{8,4},{9,5},{10,6},{11,7},{4,8},{5,9},... | collective-permute-start | bytes 393224 | tf_op jit(solution)/shard_map/ppermute | solution.py:239
  19.2 2.6 %collective-permute-start.10 = (f32[2,32,512]{2,1,0:T(8,128)S(1)}, f32[2,32,512]{2,1,0:T(8,128)S(1)}, u32[]{:S(2)}, u32[]{:S(2)}) collective-permute-start(f32[2,32,512]{2,1,0:T(8,128)S(1)} %get-tuple-element.43), channel_id=1, source_target_pairs={{30,0},{31,1},{28,2},{29,3},{10,4},{11,5},{8,6},{9,7},{6,8},{7,9},... | collective-permute-start | bytes 393224 | tf_op jit(solution)/shard_map/ppermute | solution.py:239
  21.8 0.0 collective-permute-done.3.rest_0_
  21.8 0.0 collective-permute-done.4.rest_1_
  21.8 1.4 %interp1.1 = (f32[2,32,512]{2,1,0:T(8,128)S(1)}, f32[2,32,512]{2,1,0:T(8,128)S(1)}, f32[32,128]{1,0:T(8,128)S(1)}) custom-call(bf16[2,512,192]{2,1,0:T(8,128)(2,1)S(1)} %get-tuple-element.25.high, bf16[2,512,192]{2,1,0:T(8,128)(2,1)S(1)} %get-tuple-element.26.low, f32[32,128]{1,0:T(8,128)S(1)} %get-tuple-element.29.carried, ...), custom_call_target="tpu_custom_call" | custom-call | flops 400000000 | bytes 1114112 | tf_op jit(solution)/shard_map/interp1/pallas_call | solution.py:204
  23.2 0.1 collective-permute-start.7
  23.3 2.0 %collective-permute-start.8 = (f32[2,32,512]{2,1,0:T(8,128)S(1)}, f32[2,32,512]{2,1,0:T(8,128)S(1)}, u32[]{:S(2)}, u32[]{:S(2)}) collective-permute-start(f32[2,32,512]{2,1,0:T(8,128)S(1)} %get-tuple-element.41), channel_id=1, source_target_pairs={{6,0},{7,1},{4,2},{5,3},{2,4},{3,5},{0,6},{1,7},{14,8},{15,9},{12,... | collective-permute-start | bytes 393224 | tf_op jit(solution)/shard_map/ppermute | solution.py:239
  25.2 0.0 collective-permute-done.5.rest_1_
  25.2 2.1 %interp2.1 = (f32[2,32,512]{2,1,0:T(8,128)S(1)}, f32[2,32,512]{2,1,0:T(8,128)S(1)}, f32[32,128]{1,0:T(8,128)}) custom-call(bf16[2,512,192]{2,1,0:T(8,128)(2,1)S(1)} %get-tuple-element.25.high, bf16[2,512,192]{2,1,0:T(8,128)(2,1)S(1)} %get-tuple-element.26.low, f32[32,128]{1,0:T(8,128)S(1)} %get-tuple-element.32.carried, ...), custom_call_target="tpu_custom_call" | custom-call | flops 400000000 | bytes 1130496 | tf_op jit(solution)/shard_map/interp2/pallas_call | solution.py:204
  27.3 1.5 %collective-permute-start.6 = (f32[2,32,512]{2,1,0:T(8,128)S(1)}, f32[2,32,512]{2,1,0:T(8,128)S(1)}, u32[]{:S(2)}, u32[]{:S(2)}) collective-permute-start(f32[2,32,512]{2,1,0:T(8,128)S(1)} %get-tuple-element.37), channel_id=1, source_target_pairs={{2,0},{3,1},{0,2},{1,3},{6,4},{7,5},{4,6},{5,7},{10,8},{11,9},{8,1... | collective-permute-start | bytes 393224 | tf_op jit(solution)/shard_map/ppermute | solution.py:239
  28.8 3.4 %all-to-all-start = ((f32[32,1,128]{2,1,0:T(1,128)}), f32[32,1,128]{2,1,0:T(1,128)S(1)}, u32[]{:S(2)}, u32[]{:S(2)}) async-start(f32[32,1,128]{2,1,0:T(1,128)} %bitcast.6), calls=%async_computation | async-start | bytes 32768 | tf_op jit(solution)/shard_map/all_to_all | solution.py:287
  32.2 0.0 collective-permute-done.9.rest_0_
  32.2 0.0 collective-permute-done.10.rest_1_
  32.3 1.3 %scatter0.1.rest_4_ = f32[512,192]{1,0:T(8,128)S(1)} custom-call(f32[2,32,512]{2,1,0:T(8,128)S(1)} %collective-permute-done.9.rest_0_, f32[2,32,512]{2,1,0:T(8,128)S(1)} %collective-permute-done.10.rest_1_, s32[3,4,512]{2,1,0:T(4,128)S(1)} %get-tuple-element.38.rest_2_, s32[3,4,512]{2,1,0:T(4,128)S(1)} %get-tuple-element.39.rest_3_), custom_call_target="tpu_custom_call" | custom-call | flops 400000000 | bytes 704512 | tf_op jit(solution)/shard_map/scatter0/pallas_call | solution.py:204
  33.6 0.0 collective-permute-done.7.rest_0_
  33.6 0.0 collective-permute-done.8.rest_1_
  33.6 1.3 %scatter1.1.rest_4_ = f32[512,192]{1,0:T(8,128)S(1)} custom-call(f32[2,32,512]{2,1,0:T(8,128)S(1)} %collective-permute-done.7.rest_0_, f32[2,32,512]{2,1,0:T(8,128)S(1)} %collective-permute-done.8.rest_1_, s32[3,4,512]{2,1,0:T(4,128)S(1)} %get-tuple-element.38.rest_2_, s32[3,4,512]{2,1,0:T(4,128)S(1)} %get-tuple-element.39.rest_3_, ...), custom_call_target="tpu_custom_call" | custom-call | flops 400000000 | bytes 1097728 | tf_op jit(solution)/shard_map/scatter1/pallas_call | solution.py:204
  34.9 0.0 collective-permute-done.6.rest_1_
  34.9 1.3 %scatter2.1.carried = f32[512,192]{1,0:T(8,128)S(1)} custom-call(f32[2,32,512]{2,1,0:T(8,128)S(1)} %get-tuple-element.36.rest_0_, f32[2,32,512]{2,1,0:T(8,128)S(1)} %collective-permute-done.6.rest_1_, s32[3,4,512]{2,1,0:T(4,128)S(1)} %get-tuple-element.38.rest_2_, s32[3,4,512]{2,1,0:T(4,128)S(1)} %get-tuple-element.39.rest_3_, f32[512,192]{1,0:T(8,128)S(1)} %scatter1.1.rest_4_), custom_call_target="tpu_custom_call" | custom-call | flops 400000000 | bytes 1097728 | tf_op jit(solution)/shard_map/scatter2/pallas_call | solution.py:204
  36.2 3.2 %all-to-all-done = f32[32,1,128]{2,1,0:T(1,128)S(1)} async-done(((f32[32,1,128]{2,1,0:T(1,128)}), f32[32,1,128]{2,1,0:T(1,128)S(1)}, u32[]{:S(2)}, u32[]{:S(2)}) %all-to-all-start) | async-done | bytes 16416 | tf_op jit(solution)/shard_map/all_to_all | solution.py:287
  39.3 0.9 %scale.1 = f32[512,192]{1,0:T(8,128)} custom-call(f32[512,192]{1,0:T(8,128)S(1)} %scatter2.1.carried, f32[32,128]{1,0:T(8,128)S(1)} %bitcast.10), custom_call_target="tpu_custom_call" | custom-call | flops 1000000 | bytes 802816 | tf_op jit(solution)/shard_map/scale/pallas_call | solution.py:204
  (1 shorter events, 0.0 us)
Async XLA Ops:
  0.0 10.3 %collective-permute-start = (f32[512,192]{1,0:T(8,128)}, f32[512,192]{1,0:T(8,128)S(1)}, u32[]{:S(2)}, u32[]{:S(2)}) collective-permute-start(f32[512,192]{1,0:T(8,128)} %bitcast.11), channel_id=1, source_target_pairs={{0,1},{1,0},{2,3},{3,2},{4,5},{5,4},{6,7},{7,6},{8,9},{9,8},{10,11... | collective-permute-start | bytes 1179656 | tf_op jit(solution)/shard_map/ppermute | solution.py:264
  1.7 11.4 %collective-permute-start.1 = (f32[2,4,512]{2,1,0:T(4,128)S(1)}, f32[2,4,512]{2,1,0:T(4,128)S(1)}, u32[]{:S(2)}, u32[]{:S(2)}) collective-permute-start(f32[2,4,512]{2,1,0:T(4,128)S(1)} %get-tuple-element.27), channel_id=1, source_target_pairs={{0,28},{1,29},{2,30},{3,31},{4,8},{5,9},{6,10},{7,11},{8,4},{9,5},... | collective-permute-start | bytes 49160 | tf_op jit(solution)/shard_map/ppermute | solution.py:239
  7.3 7.3 %collective-permute-start.2 = (f32[2,4,512]{2,1,0:T(4,128)S(1)}, f32[2,4,512]{2,1,0:T(4,128)S(1)}, u32[]{:S(2)}, u32[]{:S(2)}) collective-permute-start(f32[2,4,512]{2,1,0:T(4,128)S(1)} %get-tuple-element.28), channel_id=1, source_target_pairs={{0,30},{1,31},{2,28},{3,29},{4,10},{5,11},{6,8},{7,9},{8,6},{9,7},... | collective-permute-start | bytes 49160 | tf_op jit(solution)/shard_map/ppermute | solution.py:239
  8.4 13.4 %collective-permute-start.3 = (f32[2,4,512]{2,1,0:T(4,128)S(1)}, f32[2,4,512]{2,1,0:T(4,128)S(1)}, u32[]{:S(2)}, u32[]{:S(2)}) collective-permute-start(f32[2,4,512]{2,1,0:T(4,128)S(1)} %get-tuple-element.30), channel_id=1, source_target_pairs={{0,4},{1,5},{2,6},{3,7},{4,0},{5,1},{6,2},{7,3},{8,12},{9,13},{10,... | collective-permute-start | bytes 49160 | tf_op jit(solution)/shard_map/ppermute | solution.py:239
  8.4 13.4 %collective-permute-start.4 = (f32[2,4,512]{2,1,0:T(4,128)S(1)}, f32[2,4,512]{2,1,0:T(4,128)S(1)}, u32[]{:S(2)}, u32[]{:S(2)}) collective-permute-start(f32[2,4,512]{2,1,0:T(4,128)S(1)} %get-tuple-element.31), channel_id=1, source_target_pairs={{0,6},{1,7},{2,4},{3,5},{4,2},{5,3},{6,0},{7,1},{8,14},{9,15},{10,... | collective-permute-start | bytes 49160 | tf_op jit(solution)/shard_map/ppermute | solution.py:239
  10.3 15.0 %collective-permute-start.5 = (f32[2,4,512]{2,1,0:T(4,128)S(1)}, f32[2,4,512]{2,1,0:T(4,128)S(1)}, u32[]{:S(2)}, u32[]{:S(2)}) collective-permute-start(f32[2,4,512]{2,1,0:T(4,128)S(1)} %get-tuple-element.34), channel_id=1, source_target_pairs={{0,2},{1,3},{2,0},{3,1},{4,6},{5,7},{6,4},{7,5},{8,10},{9,11},{10,... | collective-permute-start | bytes 49160 | tf_op jit(solution)/shard_map/ppermute | solution.py:239
  16.0 16.2 %collective-permute-start.9 = (f32[2,32,512]{2,1,0:T(8,128)S(1)}, f32[2,32,512]{2,1,0:T(8,128)S(1)}, u32[]{:S(2)}, u32[]{:S(2)}) collective-permute-start(f32[2,32,512]{2,1,0:T(8,128)S(1)} %get-tuple-element.42), channel_id=1, source_target_pairs={{28,0},{29,1},{30,2},{31,3},{8,4},{9,5},{10,6},{11,7},{4,8},{5,9},... | collective-permute-start | bytes 393224 | tf_op jit(solution)/shard_map/ppermute | solution.py:239
  19.2 13.1 %collective-permute-start.10 = (f32[2,32,512]{2,1,0:T(8,128)S(1)}, f32[2,32,512]{2,1,0:T(8,128)S(1)}, u32[]{:S(2)}, u32[]{:S(2)}) collective-permute-start(f32[2,32,512]{2,1,0:T(8,128)S(1)} %get-tuple-element.43), channel_id=1, source_target_pairs={{30,0},{31,1},{28,2},{29,3},{10,4},{11,5},{8,6},{9,7},{6,8},{7,9},... | collective-permute-start | bytes 393224 | tf_op jit(solution)/shard_map/ppermute | solution.py:239
  23.2 10.4 %collective-permute-start.7 = (f32[2,32,512]{2,1,0:T(8,128)S(1)}, f32[2,32,512]{2,1,0:T(8,128)S(1)}, u32[]{:S(2)}, u32[]{:S(2)}) collective-permute-start(f32[2,32,512]{2,1,0:T(8,128)S(1)} %get-tuple-element.40), channel_id=1, source_target_pairs={{4,0},{5,1},{6,2},{7,3},{0,4},{1,5},{2,6},{3,7},{12,8},{13,9},{14,... | collective-permute-start | bytes 393224 | tf_op jit(solution)/shard_map/ppermute | solution.py:239
  23.3 10.3 %collective-permute-start.8 = (f32[2,32,512]{2,1,0:T(8,128)S(1)}, f32[2,32,512]{2,1,0:T(8,128)S(1)}, u32[]{:S(2)}, u32[]{:S(2)}) collective-permute-start(f32[2,32,512]{2,1,0:T(8,128)S(1)} %get-tuple-element.41), channel_id=1, source_target_pairs={{6,0},{7,1},{4,2},{5,3},{2,4},{3,5},{0,6},{1,7},{14,8},{15,9},{12,... | collective-permute-start | bytes 393224 | tf_op jit(solution)/shard_map/ppermute | solution.py:239
  27.3 7.5 %collective-permute-start.6 = (f32[2,32,512]{2,1,0:T(8,128)S(1)}, f32[2,32,512]{2,1,0:T(8,128)S(1)}, u32[]{:S(2)}, u32[]{:S(2)}) collective-permute-start(f32[2,32,512]{2,1,0:T(8,128)S(1)} %get-tuple-element.37), channel_id=1, source_target_pairs={{2,0},{3,1},{0,2},{1,3},{6,4},{7,5},{4,6},{5,7},{10,8},{11,9},{8,1... | collective-permute-start | bytes 393224 | tf_op jit(solution)/shard_map/ppermute | solution.py:239
  28.8 10.5 %all-to-all-start = ((f32[32,1,128]{2,1,0:T(1,128)}), f32[32,1,128]{2,1,0:T(1,128)S(1)}, u32[]{:S(2)}, u32[]{:S(2)}) async-start(f32[32,1,128]{2,1,0:T(1,128)} %bitcast.6), calls=%async_computation | async-start | bytes 32768 | tf_op jit(solution)/shard_map/all_to_all | solution.py:287

commit v3 on v2

v3 whole, which is shorter than its diff:
```python
import functools

import jax
import jax.numpy as jnp
from jax import lax
from jax.experimental import pallas as pl
from jax.experimental.pallas import tpu as pltpu
from jax.sharding import PartitionSpec as P


NODE_COORD = (-1.0, -0.4472135954999579, 0.4472135954999579, 1.0)
NODE_WEIGHT = (1.0 / 6.0, 5.0 / 6.0, 5.0 / 6.0, 1.0 / 6.0)
LANES = 128
VMEM = pltpu.MemorySpace.VMEM
HBM = pltpu.MemorySpace.HBM
FAR, NEAR, OWN = 0, 1, 2
SCATTERS = (((OWN, 0), (OWN, 2)), ((FAR, 0), (NEAR, 0)), ((FAR, 2), (NEAR, 2)))


def lagrange(coordinate):
    basis_values = []
    for row_node in range(4):
        weighted = jnp.ones_like(coordinate)
        for other_node in range(4):
            if other_node != row_node:
                weighted = weighted * (
                    (coordinate - NODE_COORD[other_node])
                    * (1.0 / (NODE_COORD[row_node] - NODE_COORD[other_node]))
                )
        basis_values.append(weighted)
    return basis_values


def bf16_parts(x):
    high = x.astype(jnp.bfloat16)
    low = (x - high.astype(jnp.float32)).astype(jnp.bfloat16)
    return high, low


def packed(x):
    rows, width = x.shape
    if width % LANES != LANES // 2:
        return x
    tiles = [x[:, i:i + LANES] for i in range(0, width - LANES // 2, LANES)]
    rest = x[:, width - LANES // 2:]
    return jnp.concatenate(tiles + [jnp.concatenate([rest[:rows // 2], rest[rows // 2:]], 1)], 0)


def packed_shape(rows, width):
    return (rows * width // LANES, LANES) if width % LANES == LANES // 2 else (rows, width)


def unpacked(dense, rows, width):
    if width % LANES != LANES // 2:
        return [(slice(0, rows), slice(0, width), dense)]
    parts = []
    for i in range(width // LANES):
        parts.append((slice(0, rows), slice(i * LANES, (i + 1) * LANES), dense[i * rows:(i + 1) * rows]))
    rest = dense[width // LANES * rows:]
    lanes = slice(width - LANES // 2, width)
    parts.append((slice(0, rows // 2), lanes, rest[:, :LANES // 2]))
    parts.append((slice(rows // 2, rows), lanes, rest[:, LANES // 2:]))
    return parts


def prep_kernel(counts_in, order_in, elem_in, coords_in, field_in, *rest):
    groups, capacity = elem_in.shape[1:]
    elements = field_in.shape[1]
    chips = groups // 2
    messages, rest = rest[:3], rest[3:]
    node_out, elem_out, dense, padded, starts, counts, order, elem, coords, field, sems = rest
    arrivals = [
        pltpu.make_async_copy(source, target, sems.at[i])
        for i, (source, target) in enumerate(
            (
                (counts_in, counts), (order_in, order), (elem_in, elem), (coords_in, coords),
                (field_in, field),
            )
        )
    ]
    for arrival in arrivals:
        arrival.start()
    for arrival in arrivals[:4]:
        arrival.wait()
    points = order.shape[1]
    padded[:, :points] = jnp.broadcast_to(order[...], (8, points))
    offset = jnp.int32(0)
    for k in range(3 * groups):
        starts[k] = offset
        offset = offset + counts[0, k]
    odd = lax.bitwise_and(lax.axis_index("sfc"), 1)
    me = lax.axis_index("grp")
    chip, core = lax.shift_right_logical(me, 1), lax.bitwise_and(me, 1)
    sides = (2 * odd, 2 - 2 * odd, 1)
    lane = lax.broadcasted_iota(jnp.int32, (8, capacity), 1)
    width = capacity + LANES
    for stage, d in enumerate(sides):
        message = messages[stage]
        for slot in range(groups):
            h = lax.rem(chip + slot // 2, chips) * 2 + lax.bitwise_xor(core, slot % 2)
            k = d * groups + h
            first, count = starts[k], counts[0, k]
            base = pl.multiple_of(lax.shift_left(lax.shift_right_logical(first, 7), 7), LANES)
            skip = lax.bitwise_and(first, LANES - 1)
            window = padded[:, pl.ds(base, width)]
            point = pltpu.roll(window, lax.rem(width - skip, width), 1)[:, :capacity]
            used = lane < count
            node = ((point.astype(jnp.float32) + 0.5) * (1.0 / elements)).astype(jnp.int32)
            at_elem = point - node * elements
            row, column = lax.shift_right_logical(node, 2), lax.bitwise_and(node, 3)
            inner_row = (row == 1) | (row == 2)
            inner_column = (column == 1) | (column == 2)
            weight = jnp.where(inner_row, NODE_WEIGHT[1], NODE_WEIGHT[0]) * jnp.where(
                inner_column, NODE_WEIGHT[1], NODE_WEIGHT[0]
            )
            weight = jnp.where(used, weight, 0.0)
            message[slot, 0:1, :] = elem[d, pl.ds(h, 1), :].astype(jnp.float32)
            message[slot, 1:2, :] = coords[0, d, pl.ds(h, 1), :]
            message[slot, 2:3, :] = coords[1, d, pl.ds(h, 1), :]
            message[slot, 3:4, :] = weight[0:1, :]
            node_out[stage, slot:slot + 1, :] = jnp.where(used, node, -1)[0:1, :]
            elem_out[stage, slot:slot + 1, :] = jnp.where(used, at_elem, -1)[0:1, :]
    arrivals[4].wait()
    dense[...] = packed(field[...])


def split_parts(dense, high, low):
    for rows, lanes, part in unpacked(dense[...], *high.shape):
        high[rows, lanes], low[rows, lanes] = bf16_parts(part)


def split_kernel(channels, mine, other, high_out, low_out, mass_out):
    for half, dense in enumerate((mine, other)):
        split_parts(dense, high_out.at[half], low_out.at[half])
    mass = None
    for part_rows, _, part in unpacked(mine[...], *high_out.shape[1:]):
        total = None
        for node in range(part_rows.start // channels, part_rows.stop // channels):
            at = node * channels - part_rows.start
            term = part[at:at + channels, :] * (NODE_WEIGHT[node // 4] * NODE_WEIGHT[node % 4])
            total = term if total is None else total + term
        summed = jnp.sum(total, axis=1, keepdims=True)
        mass = summed if mass is None else mass + summed
    mass_out[...] = mass + jnp.zeros((channels, LANES), jnp.float32)


def answered(channels, query, high, low):
    elements, capacity = high.shape[1], query.shape[-1]
    row = lax.broadcasted_iota(jnp.int32, (elements, capacity), 0).astype(jnp.float32)
    onehot = jnp.where(row == query[0:1, :], 1.0, 0.0).astype(jnp.bfloat16)
    field = jnp.dot(high[...], onehot, preferred_element_type=jnp.float32) + jnp.dot(
        low[...], onehot, preferred_element_type=jnp.float32
    )
    along_first = lagrange(query[1:2, :])
    along_second = lagrange(query[2:3, :])
    total = least = greatest = None
    for node in range(16):
        plane = field[node * channels:(node + 1) * channels, :]
        weighted = (along_first[node // 4] * along_second[node % 4]) * plane
        if total is None:
            total, least, greatest = weighted, plane, plane
        else:
            total = total + weighted
            least = jnp.minimum(least, plane)
            greatest = jnp.maximum(greatest, plane)
    value = jnp.minimum(jnp.maximum(total, least), greatest)
    return value, lane_sums(value * query[3:4, :])


def early_kernel(channels, high, low, carried, queries, values, mass):
    new = carried[...]
    for slot in range(2):
        values[slot], part = answered(channels, queries[slot], high.at[slot], low.at[slot])
        new = new + part
    mass[...] = new


def cross_kernel(*rest):
    *denses, high, low = rest
    for i, dense in enumerate(denses):
        split_parts(dense, high.at[i], low.at[i])


def late_kernel(channels, last, high, low, carried, queries, *rest):
    if last:
        old, values, mass = rest
    else:
        values, mass = rest
    new = carried[...]
    for i in range(values.shape[0]):
        values[i], part = answered(channels, queries[i + 2], high.at[i], low.at[i])
        new = new + part
    if not last:
        mass[...] = new
        return
    new = jnp.sum(new, axis=1, keepdims=True) + jnp.zeros((channels, LANES), jnp.float32)
    lane = lax.broadcasted_iota(jnp.int32, (channels, LANES), 1)
    which = lax.broadcasted_iota(jnp.int32, (channels, LANES), 0)
    spread = jnp.where(lane == which, old[...], 0.0) + jnp.where(lane == which + channels, new, 0.0)
    mass[...] = jnp.broadcast_to(jnp.sum(spread, axis=0, keepdims=True), mass.shape)


def scatter_kernel(channels, plan, *rest):
    values, (node, elem), rest = rest[:len(plan)], rest[len(plan):len(plan) + 2], rest[len(plan) + 2:]
    *carried, out = rest
    elements, capacity = out.shape[1], elem.shape[-1]
    row = lax.broadcasted_iota(jnp.int32, (elements, capacity), 0)
    total = None
    for (stage, first), block in zip(plan, values):
        for i in range(block.shape[0]):
            slot = slice(first + i, first + i + 1)
            at_node = jnp.broadcast_to(
                node[stage, slot, :].astype(jnp.float32), (channels, capacity)
            ).astype(jnp.bfloat16)
            onehot = jnp.where(row == elem[stage, slot, :], 1.0, 0.0).astype(jnp.bfloat16)
            for part in bf16_parts(block[i]):
                zero = jnp.zeros_like(part)
                spread = jnp.concatenate(
                    [jnp.where(at_node == float(n), part, zero) for n in range(16)], 0
                )
                term = lax.dot_general(
                    spread, onehot, (((1,), (1,)), ((), ())), preferred_element_type=jnp.float32
                )
                total = term if total is None else total + term
    out[...] = total + carried[0][...] if carried else total


def lane_sums(x):
    return sum(x[:, i:i + LANES] for i in range(0, x.shape[1], LANES))


def scale_kernel(channels, carried, masses, out):
    total = jnp.sum(masses[...], axis=0, keepdims=True)
    lane = lax.broadcasted_iota(jnp.int32, (channels, LANES), 1)
    which = lax.broadcasted_iota(jnp.int32, (channels, LANES), 0)
    old = jnp.sum(jnp.where(lane == which, total, 0.0), axis=1, keepdims=True)
    new = jnp.sum(jnp.where(lane == which + channels, total, 0.0), axis=1, keepdims=True)
    ratio = old / new
    for n in range(16):
        rows = slice(n * channels, (n + 1) * channels)
        out[rows, :] = carried[rows, :] * ratio


def whole(memory=VMEM):
    return pl.BlockSpec(memory_space=memory)


def call(kernel, out_shape, *args, outside=0, scratch=(), flops=1_000_000):
    outs = out_shape if isinstance(out_shape, (list, tuple)) else [out_shape]
    moved = sum(x.size * x.dtype.itemsize for x in list(args) + list(outs))
    run = pl.pallas_call(
        kernel,
        out_shape=out_shape,
        in_specs=[whole(HBM)] * outside + [whole()] * (len(args) - outside),
        out_specs=[whole()] * len(outs) if outs is out_shape else whole(),
        scratch_shapes=list(scratch),
        compiler_params=pltpu.CompilerParams(vmem_limit_bytes=16 * 1024 * 1024),
        cost_estimate=pl.CostEstimate(flops=flops, bytes_accessed=moved, transcendentals=0),
    )
    return run(
        *[pltpu.with_memory_space_constraint(x, HBM) if i < outside else x for i, x in enumerate(args)]
    )


def local(tracers, send_counts, point_order, depart_elem, depart_coords):
    node_count, levels, tracer_count, elements = tracers.shape
    channels = levels * tracer_count
    segments, groups = lax.axis_size("sfc"), lax.axis_size("grp")
    chips = groups // 2
    devices = segments * groups
    capacity = depart_elem.shape[-1]
    rows, points = node_count * channels, node_count * elements
    f32, i32, bf16 = jnp.float32, jnp.int32, jnp.bfloat16
    shape = jax.ShapeDtypeStruct
    dense_shape = packed_shape(rows, elements)

    def sent(stage, x):
        if stage == OWN:
            return x
        pairs = [(s, (((s + 1) ^ 1) - 1) % segments if stage == FAR else s ^ 1) for s in range(segments)]
        return lax.ppermute(x, "sfc", pairs)

    *queries, node, elem, dense = call(
        prep_kernel,
        [shape((groups, 4, capacity), f32)] * 3
        + [shape((3, groups, capacity), i32)] * 2
        + [shape(dense_shape, f32)],
        send_counts.reshape(1, 3 * groups),
        point_order.reshape(1, points),
        depart_elem.reshape(3, groups, capacity),
        depart_coords.reshape(2, 3, groups, capacity),
        tracers.reshape(rows, elements),
        outside=5,
        scratch=[
            pltpu.VMEM((8, points + capacity + LANES), i32),
            pltpu.SMEM((3 * groups,), i32),
            pltpu.SMEM((1, 3 * groups), i32),
            pltpu.VMEM((1, points), i32),
            pltpu.VMEM((3, groups, capacity), i32),
            pltpu.VMEM((2, 3, groups, capacity), f32),
            pltpu.VMEM((rows, elements), f32),
            pltpu.SemaphoreType.DMA((5,)),
        ],
    )
    other_core = [(i, i ^ 1) for i in range(groups)]
    reached = []
    for hop in range(1, chips):
        reached.append(
            lax.ppermute(dense, "grp", [((i + 2 * hop) % groups, i) for i in range(groups)])
        )
    queries = [sent(stage, queries[stage]) for stage in range(3)]
    partner = lax.ppermute(dense, "grp", other_core)
    high, low, old = call(
        functools.partial(split_kernel, channels),
        [shape((2, rows, elements), bf16)] * 2 + [shape((channels, LANES), f32)],
        dense,
        partner,
    )
    new = jnp.zeros((channels, LANES), f32)
    sums = shape((channels, LANES), f32)
    early, late = [], []
    for stage in range(3):
        values, new = call(
            functools.partial(early_kernel, channels),
            [shape((2, channels, capacity), f32), sums],
            high, low, new, queries[stage],
            flops=200_000_000,
        )
        early.append(sent(stage, values))
    across = []
    for hop, x in enumerate(reached, 1):
        across += [x, lax.ppermute(x, "grp", other_core)]
    far_high, far_low = call(cross_kernel, [shape((groups - 2, rows, elements), bf16)] * 2, *across)
    for stage in range(3):
        last = stage == 2
        values, new = call(
            functools.partial(late_kernel, channels, last),
            [
                shape((groups - 2, channels, capacity), f32),
                shape((devices, LANES), f32) if last else sums,
            ],
            far_high, far_low, new, queries[stage], *([old] if last else []),
            flops=200_000_000,
        )
        late.append(sent(stage, values))
    masses = lax.all_to_all(
        new.reshape(devices, 1, LANES), ("sfc", "grp"), split_axis=0, concat_axis=0, tiled=True
    )
    so_far = []
    for plan in SCATTERS:
        blocks = [(early if first == 0 else late)[stage] for stage, first in plan]
        so_far = [
            call(
                functools.partial(scatter_kernel, channels, plan),
                shape((rows, elements), f32),
                *blocks, node, elem, *so_far,
                flops=400_000_000,
            )
        ]
    out = call(
        functools.partial(scale_kernel, channels),
        shape((rows, elements), f32),
        *so_far, masses.reshape(devices, LANES),
    )
    return out.reshape(tracers.shape)


def solution(mesh):
    in_specs = (
        P(None, None, None, ("sfc", "grp")),
        P("sfc", "grp", None),
        P("sfc", "grp", None),
        P("sfc", "grp", None, None, None),
        P("sfc", "grp", None, None, None, None),
    )
    out_specs = P(None, None, None, ("sfc", "grp"))

    return jax.shard_map(local, mesh=mesh, in_specs=in_specs, out_specs=out_specs, check_vma=False)
```

time: 40.5 us -> 45.2 us (1.12)
  waiting for transfers between devices: 4.67 us -> 15.1 us
  starting transfers between devices: 23.4 us -> 17.6 us
    ppermute x11 -> x9, waiting for transfers between devices: 1.5 us -> 11.9 us  [the longest x1 9.11 us: local(): lax.ppermute(dense, 'grp', [((i + 2 * hop) % groups, i) for i in range(gr...]
    ppermute x11 -> x9, starting transfers between devices: 20 us -> 13.5 us  [the longest x6 10.4 us: sent(): return lax.ppermute(x, 'sfc', pairs)]
    all_to_all x1, starting transfers between devices: 3.39 us -> 4.17 us  [local(): lax.all_to_all(new.reshape(devices, 1, LANES), ('sfc', 'grp'), split_axis...]
    pallas_call x9 -> x13, Pallas kernels: 12.1 us -> 12.2 us  [call(): run(*[pltpu.with_memory_space_constraint(x, HBM) if i < outside else x fo...]
  transfers between devices with their start and end apart: 12 -> 10, of which waited for: 2 -> 4; matrix products, arithmetic and copies ran while one was open for 0% -> 0% of each run, Pallas kernels for 28% -> 22%
where the time goes in v3:
time: 45.2 us; the launch traced here: 45 us
  starting transfers between devices  17.6 us (39%)
  waiting for transfers between devices  15.1 us (33%)
  Pallas kernels  12.2 us (27%)
    pallas_call x13, Pallas kernels, call(): run(*[pltpu.with_memory_space_constraint(x, HBM) if i < outside else x fo...  12.2 us
    ppermute x6, starting transfers between devices, sent(): return lax.ppermute(x, 'sfc', pairs)  10.4 us
    ppermute x1, waiting for transfers between devices, local(): lax.ppermute(dense, 'grp', [((i + 2 * hop) % groups, i) for i in range(gr...  9.11 us
    all_to_all x1, starting transfers between devices, local(): lax.all_to_all(new.reshape(devices, 1, LANES), ('sfc', 'grp'), split_axis...  4.17 us
    all_to_all x1, waiting for transfers between devices, local(): lax.all_to_all(new.reshape(devices, 1, LANES), ('sfc', 'grp'), split_axis...  3.18 us
    ppermute x1, starting transfers between devices, local(): lax.ppermute(dense, 'grp', [((i + 2 * hop) % groups, i) for i in range(gr...  3.06 us
    ppermute x6, waiting for transfers between devices, sent(): return lax.ppermute(x, 'sfc', pairs)  2.78 us
  transfers between devices with their start and end apart: 10, of which 4 were waited for; matrix products, arithmetic and copies ran while one was open for 0% of the time, Pallas kernels for 22%

profile of v3, /device:TPU:0, one launch (start us, length us, event | category | flops | bytes accessed | tf_op | source)
XLA Modules:
  0.0 45.0 jit_solution(11705671527567074386)
XLA Ops:
  0.0 1.3 %shard_map.55 = (f32[4,4,512]{2,1,0:T(4,128)S(1)}, f32[4,4,512]{2,1,0:T(4,128)S(1)}, f32[4,4,512]{2,1,0:T(4,128)S(1)}, s32[3,4,512]{2,1,0:T(4,128)S(1)}, s32[3,4...) custom-call(s32[1,12]{1,0:T(1,128)} %bitcast.15, s32[1,3072]{1,0:T(1,128)} %bitcast.14, s32[3,4,512]{2,1,0:T(4,128)} %bitcast.13, ...), custom_call_target="tpu_custom_call" | custom-call | flops 1000000 | bytes 1019952 | tf_op jit(solution)/shard_map/pallas_call | solution.py:260
  1.3 3.1 %collective-permute-start = (f32[768,128]{1,0:T(8,128)S(1)}, f32[768,128]{1,0:T(8,128)S(1)}, u32[]{:S(2)}, u32[]{:S(2)}) collective-permute-start(f32[768,128]{1,0:T(8,128)S(1)} %get-tuple-element.28.mine), channel_id=1, source_target_pairs={{2,0},{3,1},{0,2},{1,3},{6,4},{7,5},{4,6},{5,7},{10,8},{11,9},{8,1... | collective-permute-start | bytes 1179656 | tf_op jit(solution)/shard_map/ppermute | solution.py:309
  4.4 0.0 collective-permute-start.2
  4.4 9.1 %collective-permute-done.rest_0_ = f32[768,128]{1,0:T(8,128)S(1)} collective-permute-done((f32[768,128]{1,0:T(8,128)S(1)}, f32[768,128]{1,0:T(8,128)S(1)}, u32[]{:S(2)}, u32[]{:S(2)}) %collective-permute-start) | collective-permute-done | bytes 393248 | tf_op jit(solution)/shard_map/ppermute | solution.py:309
  13.5 0.0 collective-permute-start.1
  13.5 4.8 %collective-permute-start.3 = (f32[4,4,512]{2,1,0:T(4,128)S(1)}, f32[4,4,512]{2,1,0:T(4,128)S(1)}, u32[]{:S(2)}, u32[]{:S(2)}) collective-permute-start(f32[4,4,512]{2,1,0:T(4,128)S(1)} %get-tuple-element.33), channel_id=1, source_target_pairs={{0,28},{4,8},{8,4},{12,16},{16,12},{20,24},{24,20},{28,0},{1,29},{... | collective-permute-start | bytes 98312 | tf_op jit(solution)/shard_map/ppermute | solution.py:281
  18.2 0.0 collective-permute-start.4
  18.3 0.0 collective-permute-done.2.other
  18.3 0.3 shard_map.57
  18.6 1.7 %collective-permute-done.3.queries = f32[4,4,512]{2,1,0:T(4,128)S(1)} collective-permute-done((f32[4,4,512]{2,1,0:T(4,128)S(1)}, f32[4,4,512]{2,1,0:T(4,128)S(1)}, u32[]{:S(2)}, u32[]{:S(2)}) %collective-permute-start.3) | collective-permute-done | bytes 32800 | tf_op jit(solution)/shard_map/ppermute | solution.py:281
  20.3 0.8 %shard_map.58 = (f32[2,32,512]{2,1,0:T(8,128)S(1)}, f32[32,128]{1,0:T(8,128)S(1)}) custom-call(bf16[2,512,192]{2,1,0:T(8,128)(2,1)S(1)} %get-tuple-element.31.high, bf16[2,512,192]{2,1,0:T(8,128)(2,1)S(1)} %get-tuple-element.32.low, f32[32,128]{1,0:T(8,128)S(1)} %broadcast_in_dim.3.carried, f32[4,4,512]{2,1,0:T(4,128)S(1)} %collective-permute-done.3.queries), custom_call_target="tpu_custom_call" | custom-call | flops 200000000 | bytes 983040 | tf_op jit(solution)/shard_map/pallas_call | solution.py:260
  21.1 1.1 %collective-permute-done.4.queries = f32[4,4,512]{2,1,0:T(4,128)S(1)} collective-permute-done((f32[4,4,512]{2,1,0:T(4,128)S(1)}, f32[4,4,512]{2,1,0:T(4,128)S(1)}, u32[]{:S(2)}, u32[]{:S(2)}) %collective-permute-start.4) | collective-permute-done | bytes 32800 | tf_op jit(solution)/shard_map/ppermute | solution.py:281
  22.2 0.8 %shard_map.59 = (f32[2,32,512]{2,1,0:T(8,128)S(1)}, f32[32,128]{1,0:T(8,128)S(1)}) custom-call(bf16[2,512,192]{2,1,0:T(8,128)(2,1)S(1)} %get-tuple-element.31.high, bf16[2,512,192]{2,1,0:T(8,128)(2,1)S(1)} %get-tuple-element.32.low, f32[32,128]{1,0:T(8,128)S(1)} %get-tuple-element.34.carried, f32[4,4,512]{2,1,0:T(4,128)S(1)} %collective-permute-done.4.queries), custom_call_target="tpu_custom_call" | custom-call | flops 200000000 | bytes 983040 | tf_op jit(solution)/shard_map/pallas_call | solution.py:260
  23.0 0.1 collective-permute-start.8
  23.0 3.6 %collective-permute-start.7 = (f32[2,32,512]{2,1,0:T(8,128)S(1)}, f32[2,32,512]{2,1,0:T(8,128)S(1)}, u32[]{:S(2)}, u32[]{:S(2)}) collective-permute-start(f32[2,32,512]{2,1,0:T(8,128)S(1)} %get-tuple-element.44), channel_id=1, source_target_pairs={{0,28},{4,8},{8,4},{12,16},{16,12},{20,24},{24,20},{28,0},{1,29},{... | collective-permute-start | bytes 393224 | tf_op jit(solution)/shard_map/ppermute | solution.py:281
  26.6 0.8 %shard_map.60 = (f32[2,32,512]{2,1,0:T(8,128)S(1)}, f32[32,128]{1,0:T(8,128)S(1)}) custom-call(bf16[2,512,192]{2,1,0:T(8,128)(2,1)S(1)} %get-tuple-element.31.high, bf16[2,512,192]{2,1,0:T(8,128)(2,1)S(1)} %get-tuple-element.32.low, f32[32,128]{1,0:T(8,128)S(1)} %get-tuple-element.36.carried, f32[4,4,512]{2,1,0:T(4,128)S(1)} %get-tuple-element.37.queries), custom_call_target="tpu_custom_call" | custom-call | flops 200000000 | bytes 983040 | tf_op jit(solution)/shard_map/pallas_call | solution.py:260
  27.4 0.0 collective-permute-done.1.rest_1_
  27.4 0.3 shard_map.56
  27.7 0.8 %shard_map.61 = (f32[2,32,512]{2,1,0:T(8,128)S(1)}, f32[32,128]{1,0:T(8,128)S(1)}) custom-call(bf16[2,512,192]{2,1,0:T(8,128)(2,1)S(1)} %get-tuple-element.29.high, bf16[2,512,192]{2,1,0:T(8,128)(2,1)S(1)} %get-tuple-element.30.low, f32[32,128]{1,0:T(8,128)S(1)} %get-tuple-element.38.carried, f32[4,4,512]{2,1,0:T(4,128)S(1)} %collective-permute-done.3.queries), custom_call_target="tpu_custom_call" | custom-call | flops 200000000 | bytes 983040 | tf_op jit(solution)/shard_map/pallas_call | solution.py:260
  28.5 0.8 %shard_map.62 = (f32[2,32,512]{2,1,0:T(8,128)S(1)}, f32[32,128]{1,0:T(8,128)S(1)}) custom-call(bf16[2,512,192]{2,1,0:T(8,128)(2,1)S(1)} %get-tuple-element.29.high, bf16[2,512,192]{2,1,0:T(8,128)(2,1)S(1)} %get-tuple-element.30.low, f32[32,128]{1,0:T(8,128)S(1)} %get-tuple-element.40.carried, f32[4,4,512]{2,1,0:T(4,128)S(1)} %collective-permute-done.4.queries), custom_call_target="tpu_custom_call" | custom-call | flops 200000000 | bytes 983040 | tf_op jit(solution)/shard_map/pallas_call | solution.py:260
  29.3 0.1 collective-permute-start.6
  29.4 1.9 %collective-permute-start.5 = (f32[2,32,512]{2,1,0:T(8,128)S(1)}, f32[2,32,512]{2,1,0:T(8,128)S(1)}, u32[]{:S(2)}, u32[]{:S(2)}) collective-permute-start(f32[2,32,512]{2,1,0:T(8,128)S(1)} %get-tuple-element.39), channel_id=1, source_target_pairs={{0,28},{4,8},{8,4},{12,16},{16,12},{20,24},{24,20},{28,0},{1,29},{... | collective-permute-start | bytes 393224 | tf_op jit(solution)/shard_map/ppermute | solution.py:281
  31.3 1.5 %shard_map.63 = (f32[2,32,512]{2,1,0:T(8,128)S(1)}, f32[32,128]{1,0:T(8,128)}) custom-call(bf16[2,512,192]{2,1,0:T(8,128)(2,1)S(1)} %get-tuple-element.29.high, bf16[2,512,192]{2,1,0:T(8,128)(2,1)S(1)} %get-tuple-element.30.low, f32[32,128]{1,0:T(8,128)S(1)} %get-tuple-element.47.carried, f32[4,4,512]{2,1,0:T(4,128)S(1)} %get-tuple-element.37.queries, ...), custom_call_target="tpu_custom_call" | custom-call | flops 200000000 | bytes 999424 | tf_op jit(solution)/shard_map/pallas_call | solution.py:260
  32.8 4.2 %all-to-all-start = ((f32[32,1,128]{2,1,0:T(1,128)}), f32[32,1,128]{2,1,0:T(1,128)S(1)}, u32[]{:S(2)}, u32[]{:S(2)}) async-start(f32[32,1,128]{2,1,0:T(1,128)} %bitcast.6), calls=%async_computation | async-start | bytes 32768 | tf_op jit(solution)/shard_map/all_to_all | solution.py:346
  37.0 1.3 %shard_map.64.rest_4_ = f32[512,192]{1,0:T(8,128)S(1)} custom-call(f32[2,32,512]{2,1,0:T(8,128)S(1)} %get-tuple-element.46.rest_0_, f32[2,32,512]{2,1,0:T(8,128)S(1)} %get-tuple-element.49.rest_1_, s32[3,4,512]{2,1,0:T(4,128)S(1)} %get-tuple-element.42.rest_2_, s32[3,4,512]{2,1,0:T(4,128)S(1)} %get-tuple-element.43.rest_3_), custom_call_target="tpu_custom_call" | custom-call | flops 400000000 | bytes 704512 | tf_op jit(solution)/shard_map/pallas_call | solution.py:260
  38.3 0.0 collective-permute-done.8.rest_1_
  38.3 0.0 collective-permute-done.7.rest_0_
  38.3 1.3 %shard_map.65.rest_4_ = f32[512,192]{1,0:T(8,128)S(1)} custom-call(f32[2,32,512]{2,1,0:T(8,128)S(1)} %collective-permute-done.7.rest_0_, f32[2,32,512]{2,1,0:T(8,128)S(1)} %collective-permute-done.8.rest_1_, s32[3,4,512]{2,1,0:T(4,128)S(1)} %get-tuple-element.42.rest_2_, s32[3,4,512]{2,1,0:T(4,128)S(1)} %get-tuple-element.43.rest_3_, ...), custom_call_target="tpu_custom_call" | custom-call | flops 400000000 | bytes 1097728 | tf_op jit(solution)/shard_map/pallas_call | solution.py:260
  39.6 0.0 collective-permute-done.6.rest_1_
  39.6 0.0 collective-permute-done.5.rest_0_
  39.6 1.3 %shard_map.66.carried = f32[512,192]{1,0:T(8,128)S(1)} custom-call(f32[2,32,512]{2,1,0:T(8,128)S(1)} %collective-permute-done.5.rest_0_, f32[2,32,512]{2,1,0:T(8,128)S(1)} %collective-permute-done.6.rest_1_, s32[3,4,512]{2,1,0:T(4,128)S(1)} %get-tuple-element.42.rest_2_, s32[3,4,512]{2,1,0:T(4,128)S(1)} %get-tuple-element.43.rest_3_, ...), custom_call_target="tpu_custom_call" | custom-call | flops 400000000 | bytes 1097728 | tf_op jit(solution)/shard_map/pallas_call | solution.py:260
  40.9 3.2 %all-to-all-done = f32[32,1,128]{2,1,0:T(1,128)S(1)} async-done(((f32[32,1,128]{2,1,0:T(1,128)}), f32[32,1,128]{2,1,0:T(1,128)S(1)}, u32[]{:S(2)}, u32[]{:S(2)}) %all-to-all-start) | async-done | bytes 16416 | tf_op jit(solution)/shard_map/all_to_all | solution.py:346
  44.1 0.9 %shard_map.67 = f32[512,192]{1,0:T(8,128)} custom-call(f32[512,192]{1,0:T(8,128)S(1)} %shard_map.66.carried, f32[32,128]{1,0:T(8,128)S(1)} %bitcast.10), custom_call_target="tpu_custom_call" | custom-call | flops 1000000 | bytes 802816 | tf_op jit(solution)/shard_map/pallas_call | solution.py:260
  (1 shorter events, 0.0 us)
Async XLA Ops:
  1.3 12.2 %collective-permute-start = (f32[768,128]{1,0:T(8,128)S(1)}, f32[768,128]{1,0:T(8,128)S(1)}, u32[]{:S(2)}, u32[]{:S(2)}) collective-permute-start(f32[768,128]{1,0:T(8,128)S(1)} %get-tuple-element.28.mine), channel_id=1, source_target_pairs={{2,0},{3,1},{0,2},{1,3},{6,4},{7,5},{4,6},{5,7},{10,8},{11,9},{8,1... | collective-permute-start | bytes 1179656 | tf_op jit(solution)/shard_map/ppermute | solution.py:309
  4.4 13.9 %collective-permute-start.2 = (f32[768,128]{1,0:T(8,128)S(1)}, f32[768,128]{1,0:T(8,128)S(1)}, u32[]{:S(2)}, u32[]{:S(2)}) collective-permute-start(f32[768,128]{1,0:T(8,128)S(1)} %get-tuple-element.28.mine), channel_id=1, source_target_pairs={{0,1},{1,0},{2,3},{3,2},{4,5},{5,4},{6,7},{7,6},{8,9},{9,8},{10,11... | collective-permute-start | bytes 1179656 | tf_op jit(solution)/shard_map/ppermute | solution.py:312
  13.5 13.9 %collective-permute-start.1 = (f32[768,128]{1,0:T(8,128)S(1)}, f32[768,128]{1,0:T(8,128)S(1)}, u32[]{:S(2)}, u32[]{:S(2)}) collective-permute-start(f32[768,128]{1,0:T(8,128)S(1)} %collective-permute-done.rest_0_), channel_id=1, source_target_pairs={{0,1},{1,0},{2,3},{3,2},{4,5},{5,4},{6,7},{7,6},{8,9},{9,8},{10,11... | collective-permute-start | bytes 1179656 | tf_op jit(solution)/shard_map/ppermute | solution.py:332
  13.5 6.8 %collective-permute-start.3 = (f32[4,4,512]{2,1,0:T(4,128)S(1)}, f32[4,4,512]{2,1,0:T(4,128)S(1)}, u32[]{:S(2)}, u32[]{:S(2)}) collective-permute-start(f32[4,4,512]{2,1,0:T(4,128)S(1)} %get-tuple-element.33), channel_id=1, source_target_pairs={{0,28},{4,8},{8,4},{12,16},{16,12},{20,24},{24,20},{28,0},{1,29},{... | collective-permute-start | bytes 98312 | tf_op jit(solution)/shard_map/ppermute | solution.py:281
  18.2 3.9 %collective-permute-start.4 = (f32[4,4,512]{2,1,0:T(4,128)S(1)}, f32[4,4,512]{2,1,0:T(4,128)S(1)}, u32[]{:S(2)}, u32[]{:S(2)}) collective-permute-start(f32[4,4,512]{2,1,0:T(4,128)S(1)} %get-tuple-element.35), channel_id=1, source_target_pairs={{0,4},{4,0},{8,12},{12,8},{16,20},{20,16},{24,28},{28,24},{1,5},{5... | collective-permute-start | bytes 98312 | tf_op jit(solution)/shard_map/ppermute | solution.py:281
  23.0 15.3 %collective-permute-start.8 = (f32[2,32,512]{2,1,0:T(8,128)S(1)}, f32[2,32,512]{2,1,0:T(8,128)S(1)}, u32[]{:S(2)}, u32[]{:S(2)}) collective-permute-start(f32[2,32,512]{2,1,0:T(8,128)S(1)} %get-tuple-element.45), channel_id=1, source_target_pairs={{0,4},{4,0},{8,12},{12,8},{16,20},{20,16},{24,28},{28,24},{1,5},{5... | collective-permute-start | bytes 393224 | tf_op jit(solution)/shard_map/ppermute | solution.py:281
  23.0 15.3 %collective-permute-start.7 = (f32[2,32,512]{2,1,0:T(8,128)S(1)}, f32[2,32,512]{2,1,0:T(8,128)S(1)}, u32[]{:S(2)}, u32[]{:S(2)}) collective-permute-start(f32[2,32,512]{2,1,0:T(8,128)S(1)} %get-tuple-element.44), channel_id=1, source_target_pairs={{0,28},{4,8},{8,4},{12,16},{16,12},{20,24},{24,20},{28,0},{1,29},{... | collective-permute-start | bytes 393224 | tf_op jit(solution)/shard_map/ppermute | solution.py:281
  29.3 10.3 %collective-permute-start.6 = (f32[2,32,512]{2,1,0:T(8,128)S(1)}, f32[2,32,512]{2,1,0:T(8,128)S(1)}, u32[]{:S(2)}, u32[]{:S(2)}) collective-permute-start(f32[2,32,512]{2,1,0:T(8,128)S(1)} %get-tuple-element.41), channel_id=1, source_target_pairs={{0,4},{4,0},{8,12},{12,8},{16,20},{20,16},{24,28},{28,24},{1,5},{5... | collective-permute-start | bytes 393224 | tf_op jit(solution)/shard_map/ppermute | solution.py:281
  29.4 10.2 %collective-permute-start.5 = (f32[2,32,512]{2,1,0:T(8,128)S(1)}, f32[2,32,512]{2,1,0:T(8,128)S(1)}, u32[]{:S(2)}, u32[]{:S(2)}) collective-permute-start(f32[2,32,512]{2,1,0:T(8,128)S(1)} %get-tuple-element.39), channel_id=1, source_target_pairs={{0,28},{4,8},{8,4},{12,16},{16,12},{20,24},{24,20},{28,0},{1,29},{... | collective-permute-start | bytes 393224 | tf_op jit(solution)/shard_map/ppermute | solution.py:281
  32.8 11.3 %all-to-all-start = ((f32[32,1,128]{2,1,0:T(1,128)}), f32[32,1,128]{2,1,0:T(1,128)S(1)}, u32[]{:S(2)}, u32[]{:S(2)}) async-start(f32[32,1,128]{2,1,0:T(1,128)} %bitcast.6), calls=%async_computation | async-start | bytes 32768 | tf_op jit(solution)/shard_map/all_to_all | solution.py:346
